TPU v7x, 128 devices: a whole 4x4x4 slice. The times are simulated.
128 devices in a mesh: cat: 2 (over x_hi), lat: 4 (over x_lo, core), lon: 16 (over z, y).
Axes of the slice: x: 4 (x_hi: 2, x_lo: 2; x = x_hi * 2 + x_lo), y: 4, z: 4, core: 2. Of those that a mesh axis runs over, the one named last changes fastest.
Arguments:
- thickness: bfloat16 [40, 1024, 10240], P('cat', 'lat', 'lon'), may hold values from 0.099609375 to 4
- area: bfloat16 [40, 1024, 10240], P('cat', 'lat', 'lon'), may hold values from 0.0049743652 to 0.049804688
- ridge_weight: float32 [40], P('cat'), may hold values from 0.2 to 2
- cat_top: int32 [1024, 10240], P('lat', 'lon'), may hold values from 1 to 40
- land_mask: int32 [1024, 10240], P('lat', 'lon'), may hold values 0 or 1
- velocity_u: float32 [1024, 10240], P('lat', 'lon'), may hold values from -1.8 to 1.8
- velocity_v: float32 [1024, 10240], P('lat', 'lon'), may hold values from -1.8 to 1.8
- stress_div: float32 [1024, 10240], P('lat', 'lon'), may hold values from -3 to 3
- stress_ten: float32 [1024, 10240], P('lat', 'lon'), may hold values from -3 to 3
- stress_shear: float32 [1024, 10240], P('lat', 'lon'), may hold values from -3 to 3
- wind_x: float32 [1024, 10240], P('lat', 'lon'), may hold values from -6 to 6
- wind_y: float32 [1024, 10240], P('lat', 'lon'), may hold values from -6 to 6
- water_drag: float32 [1024, 10240], P('lat', 'lon'), may hold values from 0.2 to 2
Outputs:
- new_u: float32 [1024, 10240], P('lat', 'lon')
- new_v: float32 [1024, 10240], P('lat', 'lon')
- new_div: float32 [1024, 10240], P('lat', 'lon')
- new_ten: float32 [1024, 10240], P('lat', 'lon')
- new_shear: float32 [1024, 10240], P('lat', 'lon')
Inputs may be any that keep to these rules, and one draw needn't show every extreme that they name: Categories with index cat_top or above are absent from a cell.
All inputs are finite; a program needn't handle non-finite values. No bound on the sum of `land_mask` on one device may be relied on, other than what follows from the above.
Results may differ from a plain program's by a relative error of at most 0.0003.
Values sent between devices are 32-bit elements; how exact they have to be, the bound alone decides.
A program may use at most 128 MiB of HBM per device.

v0:
```python
import jax
import jax.numpy as jnp
from jax import lax
from jax.sharding import PartitionSpec as P

SUB = 4


ELASTIC = 2.0
ECC_SQUARED = 4.0
DELTA_FLOOR = 0.05
CORIOLIS = 0.5


def from_everyone(x, axis):
    count = lax.axis_size(axis)
    return lax.all_to_all(jnp.broadcast_to(x[None], (count, *x.shape)), axis, 0, 0, tiled=True)


def over_copies(x, axis):
    return from_everyone(x, axis).sum(axis=0)


def together(arrays, axis):
    ends = [0]
    for a in arrays:
        ends.append(ends[-1] + a.size)
    subtotal = over_copies(jnp.concatenate([a.ravel() for a in arrays]), axis)
    return tuple((subtotal[b:e].reshape(a.shape) for a, b, e in zip(arrays, ends, ends[1:])))


def extended(cells, sides, width, closed):
    for axis, dim in sides:
        count = lax.axis_size(axis)
        ends = count if closed else count - 1
        head = lax.slice_in_dim(cells, 0, width, axis=dim)
        tail = lax.slice_in_dim(cells, cells.shape[dim] - width, cells.shape[dim], axis=dim)
        cells = jnp.concatenate(
            [
                lax.ppermute(tail, axis, [(i, (i + 1) % count) for i in range(ends)]),
                cells,
                lax.ppermute(head, axis, [((i + 1) % count, i) for i in range(ends)]),
            ],
            axis=dim,
        )
    return cells


def slopes(along, across):
    return (
        0.5 * (along[:, :, 2:] - along[:, :, :-2]),
        0.5 * (across[:, 2:, :] - across[:, :-2, :]),
    )


def local_pad(along_stack, across_stack):
    along = jnp.pad(along_stack, ((0, 0), (0, 0), (1, 1)))
    across = jnp.pad(across_stack, ((0, 0), (1, 1), (0, 0)))
    return (along, across)


def subcycle(velocity, stresses, statics, velocity_pad, stress_pad):
    strength, mass, concentration, drag, push_x, push_y, wet = statics
    along, across = velocity_pad(velocity, velocity)
    ddx, ddy = slopes(along, across)
    divergence = ddx[0] + ddy[1]
    tension = ddx[0] - ddy[1]
    shearing = ddy[0] + ddx[1]
    delta = jnp.sqrt(
        divergence * divergence
        + (tension * tension + shearing * shearing) / ECC_SQUARED
        + DELTA_FLOOR * DELTA_FLOOR
    )
    relax = 1.0 / (1.0 + ELASTIC)
    viscous = ELASTIC * strength / delta
    first = wet * (stresses[0] + viscous * (divergence - delta)) * relax
    second = wet * (stresses[1] + viscous * tension / ECC_SQUARED) * relax
    cross = wet * (stresses[2] + viscous * shearing / ECC_SQUARED) * relax
    normal_x = 0.5 * (first + second)
    normal_y = 0.5 * (first - second)
    along_s, across_s = stress_pad(jnp.stack([normal_x, cross]), jnp.stack([cross, normal_y]))
    sdx, sdy = slopes(along_s, across_s)
    force_x = sdx[0] + sdy[0]
    force_y = sdx[1] + sdy[1]
    denom = mass + drag + 1.0 - wet
    speed_u = (
        wet
        * (mass * velocity[0] + force_x + concentration * push_x + CORIOLIS * mass * velocity[1])
        / denom
    )
    speed_v = (
        wet
        * (mass * velocity[1] + force_y + concentration * push_y - CORIOLIS * mass * velocity[0])
        / denom
    )
    return (jnp.stack([speed_u, speed_v]), jnp.stack([first, second, cross]))


def shards(
    thickness,
    area,
    ridge_weight,
    cat_top,
    land_mask,
    velocity_u,
    velocity_v,
    stress_div,
    stress_ten,
    stress_shear,
    wind_x,
    wind_y,
    water_drag,
):
    local_cats = thickness.shape[0]
    level = lax.axis_index("cat") * local_cats + lax.broadcasted_iota(jnp.int32, thickness.shape, 0)
    present = (level < cat_top[None]).astype(jnp.float32)
    height = thickness.astype(jnp.float32)
    cover = area.astype(jnp.float32) * present
    weighted = ridge_weight[:, None, None] * cover * height * height
    strength, mass, concentration = together(
        (jnp.sum(weighted, axis=0), jnp.sum(cover * height, axis=0), jnp.sum(cover, axis=0)), "cat"
    )
    wet = land_mask.astype(jnp.float32)
    margin = 2 * SUB
    bundle = jnp.stack(
        [
            strength,
            mass,
            concentration,
            water_drag,
            wind_x,
            wind_y,
            wet,
            velocity_u,
            velocity_v,
            stress_div,
            stress_ten,
            stress_shear,
        ]
    )
    widened = extended(bundle, (("lon", 2),), margin, True)
    padded = extended(widened, (("lat", 1),), margin, False)
    statics = tuple((padded[index] for index in range(7)))
    velocity = padded[7:9]
    stresses = padded[9:12]
    for step in range(SUB):
        velocity, stresses = subcycle(velocity, stresses, statics, local_pad, local_pad)
    rows = velocity.shape[1] - margin
    cols = velocity.shape[2] - margin
    velocity = velocity[:, margin:rows, margin:cols]
    stresses = stresses[:, margin:rows, margin:cols]
    return (velocity[0], velocity[1], stresses[0], stresses[1], stresses[2])


def solution(mesh):
    return jax.shard_map(
        shards,
        mesh=mesh,
        in_specs=(
            P("cat", "lat", "lon"),
            P("cat", "lat", "lon"),
            P("cat"),
            P("lat", "lon"),
            P("lat", "lon"),
            P("lat", "lon"),
            P("lat", "lon"),
            P("lat", "lon"),
            P("lat", "lon"),
            P("lat", "lon"),
            P("lat", "lon"),
            P("lat", "lon"),
            P("lat", "lon"),
        ),
        out_specs=(
            P("lat", "lon"),
            P("lat", "lon"),
            P("lat", "lon"),
            P("lat", "lon"),
            P("lat", "lon"),
        ),
        check_vma=False,
    )
```

profile of v0, /device:TPU:1, one launch (start us, length us, event | category | flops | bytes accessed | tf_op | source)
XLA Modules:
  0.0 158.2 jit_solution(5129707785300228188)
XLA Ops:
  0.6 8.4 %fusion.1 = (f32[256,640]{1,0:T(8,128)S(1)}, f32[256,640]{1,0:T(8,128)S(1)}, f32[256,640]{1,0:T(8,128)S(1)}) fusion(bf16[20,256,640]{2,1,0:T(8,128)(2,1)} %param.13, bf16[20,256,640]{2,1,0:T(8,128)(2,1)} %param.14, s32[256,640]{1,0:T(8,128)} %param.16, f32[20]{0:T(128)} %param.15, s32[20]{0:T(128)S(1)} %iota_add_fusion), kind=kLoop, calls=%fused_computation.3 | loop fusion | flops 35553280 | bytes 15728800 | tf_op jit(solution)/shard_map/reduce_sum | solution.py:121
  9.3 9.3 %broadcast_in_dim.2 = f32[2,1,491520]{2,1,0:T(1,128)S(1)} broadcast(f32[491520]{0:T(1024)S(1)} %pad_maximum_fusion.1), dimensions={2} | broadcast | bytes 5898240 | tf_op jit(solution)/shard_map/broadcast_in_dim | solution.py:17
  18.6 49.9 %all_to_all.6 = f32[2,1,491520]{2,1,0:T(1,128)} all-to-all(f32[2,1,491520]{2,1,0:T(1,128)S(1)} %broadcast_in_dim.2), channel_id=1, replica_groups=mesh['cat'=2,'lat'=4,'lon'=16] {'cat'}, dimensions={0} | all-to-all | bytes 7864320 | tf_op jit(solution)/shard_map/all_to_all | solution.py:17
  68.5 19.4 %reduce_sum.39 = f32[491520]{0:T(1024)S(1)} reduce(f32[2,1,491520]{2,1,0:T(1,128)} %all_to_all.6, f32[]{:T(128)} %constant.31.clone.1), dimensions={0,1}, to_apply=%region_3.0 | reduce | flops 491520 | bytes 5898244 | tf_op jit(solution)/shard_map/reduce_sum | solution.py:21
  87.9 1.0 fusion.69
  88.8 1.2 slice.330
  90.5 0.9 copy-done.3
  91.5 0.2 copy-done.4
  91.7 0.2 copy-done.5
  91.9 0.7 copy-done.6
  92.7 0.1 copy-done.7
  92.9 0.2 copy-done.8
  93.1 0.7 copy-done.9
  94.0 0.2 copy-done.11
  94.3 3.1 %copy-done = f32[12,256,640]{2,1,0:T(8,128)} copy-done((f32[12,256,640]{2,1,0:T(8,128)}, f32[12,256,640]{2,1,0:T(8,128)S(1)}, u32[]{:S(2)}) %copy-start) | copy-done | bytes 7864344
  97.3 0.5 fusion.68
  97.9 0.4 copy.41
  98.3 1.3 collective-permute-start
  99.6 0.4 copy.42
  100.1 5.0 %collective-permute-start.1 = (f32[12,256,8]{1,2,0:T(8,128)S(1)}, f32[12,256,8]{1,2,0:T(8,128)S(1)}, u32[]{:S(2)}, u32[]{:S(2)}) collective-permute-start(f32[12,256,8]{1,2,0:T(8,128)S(1)} %copy.42), channel_id=1, source_target_pairs={{1,0},{2,1},{3,2},{4,3},{5,4},{6,5},{7,6},{8,7},{9,8},{10,9},{11,1... | collective-permute-start | bytes 294920 | tf_op jit(solution)/shard_map/ppermute | solution.py:42
  105.0 1.5 collective-permute-done
  106.5 0.5 copy.43
  107.0 0.5 copy.44
  107.5 1.3 pad_maximum_fusion.7
  108.8 5.5 %collective-permute-start.2 = (f32[12,8,656]{2,1,0:T(8,128)S(1)}, f32[12,8,656]{2,1,0:T(8,128)S(1)}, u32[]{:S(2)}, u32[]{:S(2)}) collective-permute-start(f32[12,8,656]{2,1,0:T(8,128)S(1)} %get-tuple-element.45), channel_id=1, source_target_pairs={{0,16},{16,32},{32,48},{1,17},{17,33},{33,49},{2,18},{18,34},{34,5... | collective-permute-start | bytes 755720 | tf_op jit(solution)/shard_map/ppermute | solution.py:40
  114.3 1.9 %collective-permute-start.3 = (f32[12,8,656]{2,1,0:T(8,128)S(1)}, f32[12,8,656]{2,1,0:T(8,128)S(1)}, u32[]{:S(2)}, u32[]{:S(2)}) collective-permute-start(f32[12,8,656]{2,1,0:T(8,128)S(1)} %get-tuple-element.46), channel_id=1, source_target_pairs={{16,0},{32,16},{48,32},{17,1},{33,17},{49,33},{18,2},{34,18},{50,3... | collective-permute-start | bytes 755720 | tf_op jit(solution)/shard_map/ppermute | solution.py:42
  116.3 1.7 %collective-permute-done.2 = f32[12,8,656]{2,1,0:T(8,128)S(1)} collective-permute-done((f32[12,8,656]{2,1,0:T(8,128)S(1)}, f32[12,8,656]{2,1,0:T(8,128)S(1)}, u32[]{:S(2)}, u32[]{:S(2)}) %collective-permute-start.2) | collective-permute-done | bytes 251936 | tf_op jit(solution)/shard_map/ppermute | solution.py:40
  118.0 4.4 %collective-permute-done.3 = f32[12,8,656]{2,1,0:T(8,128)S(1)} collective-permute-done((f32[12,8,656]{2,1,0:T(8,128)S(1)}, f32[12,8,656]{2,1,0:T(8,128)S(1)}, u32[]{:S(2)}, u32[]{:S(2)}) %collective-permute-start.3) | collective-permute-done | bytes 251936 | tf_op jit(solution)/shard_map/ppermute | solution.py:42
  122.4 6.5 %pad_maximum_fusion = f32[12,272,656]{2,1,0:T(8,128)S(1)} fusion(f32[12,8,656]{2,1,0:T(8,128)S(1)} %collective-permute-done.3, f32[12,256,8]{2,1,0:T(8,128)S(1)} %copy.44, f32[12,256,640]{2,1,0:T(8,128)} %copy-done, f32[12,256,8]{2,1,0:T(8,128)S(1)} %copy.43, f32[12,8,656]{2,1,0:T(8,128)S(1)} %collective-permute-done.2), kind=kLoop, calls=%fused_computation.6 | loop fusion | flops 8564736 | bytes 17129472 | tf_op jit(solution)/shard_map/concatenate | solution.py:38
  129.0 1.2 subtract_multiply_fusion.7
  130.2 0.9 add_multiply_fusion.3
  131.1 0.4 fusion.46
  131.5 0.5 select_maximum_fusion.7
  132.0 0.5 fusion.11
  132.7 0.2 fusion.10
  132.9 0.5 fusion.44
  133.4 0.5 fusion.37
  134.0 1.2 subtract_multiply_fusion.5
  135.2 1.6 %multiply_multiply_fusion.2 = (f32[1,272,656]{2,1,0:T(8,128)}, f32[1,272,656]{2,1,0:T(8,128)S(1)}) fusion(f32[12,272,656]{2,1,0:T(8,128)S(1)} %pad_maximum_fusion, f32[1,272,656]{2,1,0:T(8,128)S(1)} %get-tuple-element.38, f32[2,272,656]{2,1,0:T(8,128)S(1)} %get-tuple-element.68, f32[2,272,656]{2,1,0:T(8,128)S(1)} %get-tuple-element.67, ...), kind=kLoop, calls=%fused_computation.102 | loop fusion | flops 4282368 | bytes 8564736 | tf_op jit(solution)/shard_map/mul | solution.py:77
  136.8 0.9 add_multiply_fusion.2
  137.7 0.5 select_maximum_fusion.6
  138.2 0.5 fusion.9
  138.9 0.2 fusion.8
  139.2 0.6 fusion.32
  139.9 1.2 subtract_multiply_fusion.3
  141.1 1.4 multiply_multiply_fusion.1
  142.4 1.1 add_multiply_fusion.1
  143.5 0.5 select_maximum_fusion.5
  144.0 0.5 fusion.7
  144.6 0.1 select_maximum_fusion.1
  144.8 0.2 fusion.6
  145.0 0.6 fusion.22
  145.7 1.2 subtract_multiply_fusion.1
  146.9 0.9 add_multiply_fusion
  147.8 0.3 multiply_multiply_fusion.3
  148.1 1.1 slice_bitcast_fusion
  149.2 1.1 slice_bitcast_fusion.1
  150.3 0.5 select_maximum_fusion.4
  150.9 0.5 fusion.5
  151.6 0.2 fusion.4
  152.0 1.0 copy-done.1
  153.0 0.3 copy-done.2
  153.3 1.8 %fusion.53 = f32[256,640]{1,0:T(8,128)} fusion(f32[1,272,656]{2,1,0:T(8,128)S(1)} %get-tuple-element.21, f32[1,272,656]{2,1,0:T(8,128)S(1)} %get-tuple-element.23, f32[1,272,656]{2,1,0:T(8,128)S(1)} %copy-done.2, f32[1,272,656]{2,1,0:T(8,128)S(1)} %copy-done.1, f32[1,272,656]{2,1,0:T(8,128)S(1)} %get-tuple-element.47), kind=kLoop, calls=%fused_computation.147 | loop fusion | flops 1310720 | bytes 3932160 | tf_op jit(solution)/shard_map/squeeze | solution.py:152
  155.0 3.2 %fusion.59 = (f32[256,640]{1,0:T(8,128)}, f32[256,640]{1,0:T(8,128)}) fusion(f32[1,272,656]{2,1,0:T(8,128)S(1)} %get-tuple-element.34, f32[1,272,656]{2,1,0:T(8,128)S(1)} %get-tuple-element.59, f32[1,272,656]{2,1,0:T(8,128)S(1)} %get-tuple-element.57, f32[1,272,656]{2,1,0:T(8,128)S(1)} %get-tuple-element.31, f32[1,272,656]{2,1,0:T(8,128)S(1)} %get-tuple-element.40, ...), kind=kLoop, calls=%fused_computation.156 | loop fusion | flops 2621440 | bytes 9175040 | tf_op jit(solution)/shard_map/squeeze | solution.py:152
  (45 shorter events, 2.6 us)
Async XLA Ops:
  90.3 1.1 copy-start.3
  90.4 1.2 copy-start.4
  90.5 1.4 copy-start.5
  91.4 1.2 copy-start.6
  91.6 1.2 copy-start.7
  91.9 1.2 copy-start.8
  92.6 1.2 copy-start.9
  92.8 1.2 copy-start.10
  93.0 1.2 copy-start.11
  94.3 3.1 %copy-start = (f32[12,256,640]{2,1,0:T(8,128)}, f32[12,256,640]{2,1,0:T(8,128)S(1)}, u32[]{:S(2)}) copy-start(f32[12,256,640]{2,1,0:T(8,128)S(1)} %bitcast_dynamic-update-slice_fusion) | copy-start | bytes 23592964
  98.3 8.3 %collective-permute-start = (f32[12,256,8]{1,2,0:T(8,128)S(1)}, f32[12,256,8]{1,2,0:T(8,128)S(1)}, u32[]{:S(2)}, u32[]{:S(2)}) collective-permute-start(f32[12,256,8]{1,2,0:T(8,128)S(1)} %copy.41), channel_id=1, source_target_pairs={{0,1},{1,2},{2,3},{3,4},{4,5},{5,6},{6,7},{7,8},{8,9},{9,10},{10,1... | collective-permute-start | bytes 294920 | tf_op jit(solution)/shard_map/ppermute | solution.py:40
  100.1 7.0 %collective-permute-start.1 = (f32[12,256,8]{1,2,0:T(8,128)S(1)}, f32[12,256,8]{1,2,0:T(8,128)S(1)}, u32[]{:S(2)}, u32[]{:S(2)}) collective-permute-start(f32[12,256,8]{1,2,0:T(8,128)S(1)} %copy.42), channel_id=1, source_target_pairs={{1,0},{2,1},{3,2},{4,3},{5,4},{6,5},{7,6},{8,7},{9,8},{10,9},{11,1... | collective-permute-start | bytes 294920 | tf_op jit(solution)/shard_map/ppermute | solution.py:42
  108.8 9.2 %collective-permute-start.2 = (f32[12,8,656]{2,1,0:T(8,128)S(1)}, f32[12,8,656]{2,1,0:T(8,128)S(1)}, u32[]{:S(2)}, u32[]{:S(2)}) collective-permute-start(f32[12,8,656]{2,1,0:T(8,128)S(1)} %get-tuple-element.45), channel_id=1, source_target_pairs={{0,16},{16,32},{32,48},{1,17},{17,33},{33,49},{2,18},{18,34},{34,5... | collective-permute-start | bytes 755720 | tf_op jit(solution)/shard_map/ppermute | solution.py:40
  114.3 8.0 %collective-permute-start.3 = (f32[12,8,656]{2,1,0:T(8,128)S(1)}, f32[12,8,656]{2,1,0:T(8,128)S(1)}, u32[]{:S(2)}, u32[]{:S(2)}) collective-permute-start(f32[12,8,656]{2,1,0:T(8,128)S(1)} %get-tuple-element.46), channel_id=1, source_target_pairs={{16,0},{32,16},{48,32},{17,1},{33,17},{49,33},{18,2},{34,18},{50,3... | collective-permute-start | bytes 755720 | tf_op jit(solution)/shard_map/ppermute | solution.py:42
  151.8 1.2 copy-start.1
  151.9 1.4 copy-start.2
where the time goes:
time: 159 us; the launch traced here: 158 us
  other arithmetic  61.1 us (38%)
  blocking collectives  49.9 us (31%)
  local copies, waits for them, and re-layouts  24.7 us (16%)
  starting transfers between devices  13.7 us (9%)
  waiting for transfers between devices  7.63 us (5%)
    all_to_all x1, blocking collectives, from_everyone(): lax.all_to_all(jnp.broadcast_to(x[None], (count, *x.shape)), axis, 0, 0,...  49.9 us
    reduce_sum x1, other arithmetic, over_copies(): return from_everyone(x, axis).sum(axis=0)  19.4 us
    broadcast_in_dim x1, local copies, waits for them, and re-layouts, from_everyone(): jnp.broadcast_to(x[None], (count, *x.shape))  9.27 us
    reduce_sum x1, other arithmetic, shards(): jnp.sum(weighted, axis=0)  8.36 us
    unnamed x34, local copies, waits for them, and re-layouts  8.06 us
    ppermute x2, starting transfers between devices, extended(): lax.ppermute(head, axis, [((i + 1) % count, i) for i in range(ends)])  6.89 us
    ppermute x2, starting transfers between devices, extended(): lax.ppermute(tail, axis, [(i, (i + 1) % count) for i in range(ends)])  6.84 us
    mul x8, other arithmetic, slopes(): 0.5 * (along[:, :, 2:] - along[:, :, :-2])  6.78 us
  transfers between devices with their start and end apart: 4, of which 3 were waited for; matrix products, arithmetic and copies ran while one was open for 1% of the time, Pallas kernels for 0%

commit v1 on v0

v1 whole, which is shorter than its diff:
```python
import jax
import jax.numpy as jnp
from jax import lax
from jax.experimental import pallas as pl
from jax.experimental.pallas import tpu as pltpu
from jax.sharding import PartitionSpec as P

U, V, S1, S2, S12, WX, WY, DR, WT, ST, MA, CO = range(12)
NCAT = 20
ROWS = 256
COLS = 640
TILES = 5
CHUNKS = 15
AHEAD = 5
ORDER = (0, 4, 1, 2, 3)
TOP_ROW = 72
HEIGHT = 344
FIRST, LAST = 8, 41
LOADS = ((0, 16), (240, 16), (16, 48), (64, 64), (128, 64), (192, 48))
MESH = pl.DeviceIdType.MESH


def kernel(th, ar, weight, top, land, u0, v0, d0, t0, h0, wx0, wy0, dr0, out,
           F, T, A, TOP, LAND, PT, QT, LS, LR, XS, XR,
           cat_send, cat_recv, lon_send, lon_recv, edge_send, edge_recv, lat_send, lat_recv,
           load_sem, field_sem, out_sem):
    cat, lat, lon = lax.axis_index("cat"), lax.axis_index("lat"), lax.axis_index("lon")
    peer = (1 - cat, lat, lon)
    sides = ((cat, lat, lax.rem(lon + 15, 16)), (cat, lat, lax.rem(lon + 1, 16)))
    up = (cat, lax.rem(lat + 3, 4), lon)
    down = (cat, lax.rem(lat + 1, 4), lon)
    has_up, has_down = lat > 0, lat < 3

    barrier = pltpu.get_barrier_semaphore()
    for device in (peer, *sides, up, down):
        pl.semaphore_signal(barrier, inc=1, device_id=device, device_id_type=MESH)

    def load(i):
        start, size = LOADS[i]
        rows = pl.ds(start, size)
        return (
            pltpu.make_async_copy(top.at[rows, :], TOP.at[rows, :], load_sem.at[i, 0]),
            pltpu.make_async_copy(th.at[:, rows, :], T.at[:, rows, :], load_sem.at[i, 1]),
            pltpu.make_async_copy(ar.at[:, rows, :], A.at[:, rows, :], load_sem.at[i, 2]),
        )

    def field_loads():
        copies = [pltpu.make_async_copy(land, LAND, field_sem.at[8, 0])]
        for f, ref in enumerate((u0, v0, d0, t0, h0, wx0, wy0, dr0)):
            for j in range(TILES):
                copies.append(
                    pltpu.make_async_copy(
                        ref.at[:, pl.ds(j * 128, 128)], F.at[f, j, pl.ds(TOP_ROW, ROWS), :], field_sem.at[f, j]
                    )
                )
        return copies

    for i in range(3):
        for copy in load(i):
            copy.start()
    for copy in field_loads():
        copy.start()
    for i in range(3, len(LOADS)):
        for copy in load(i):
            copy.start()

    for f in range(5):
        for j in range(6):
            F[f, j, pl.ds(8 * FIRST - 8, 8), :] = jnp.zeros((8, 128), jnp.float32)
            F[f, j, pl.ds(8 * LAST + 8, 8), :] = jnp.zeros((8, 128), jnp.float32)

    @pl.when(lat == 0)
    def _():
        F[:, :, pl.ds(8 * FIRST, 8), :] = jnp.zeros((12, 6, 8, 128), jnp.float32)

    @pl.when(lat == 3)
    def _():
        F[:, :, pl.ds(8 * LAST, 8), :] = jnp.zeros((12, 6, 8, 128), jnp.float32)

    lane = lax.broadcasted_iota(jnp.int32, (8, 128), 1)
    lane16 = lax.broadcasted_iota(jnp.int32, (16, 128), 1)
    base = cat * NCAT

    def sums(block, carry):
        rows = pl.ds(pl.multiple_of(block * 16, 16), 16)
        for place, j in enumerate(ORDER):
            cols = pl.ds(j * 128, 128)
            limit = TOP[rows, cols] - base
            strength = jnp.zeros((16, 128), jnp.float32)
            mass = jnp.zeros((16, 128), jnp.float32)
            cover = jnp.zeros((16, 128), jnp.float32)
            for n in range(NCAT):
                h = T[n, rows, cols].astype(jnp.float32)
                c = A[n, rows, cols].astype(jnp.float32)
                c = jnp.where(limit > n, c, 0.0)
                m = c * h
                cover = cover + c
                mass = mass + m
                strength = strength + (weight[n] * h) * m
            PT[0, place, rows, :] = strength
            PT[1, place, rows, :] = mass
            PT[2, place, rows, :] = cover
        return carry

    def remote(src, dst, send, recv, device):
        return pltpu.make_async_remote_copy(
            src_ref=src, dst_ref=dst, send_sem=send, recv_sem=recv, device_id=device, device_id_type=MESH
        )

    def cat_message(tiles, rows, k):
        where = (slice(None), tiles, rows, slice(None))
        return remote(PT.at[where], QT.at[where], cat_send.at[k], cat_recv.at[k], peer)

    def border(c):
        return cat_message(pl.ds(0, 2), pl.ds(pl.multiple_of(8 + c * 16, 8), 16), c)

    def inner(c):
        return cat_message(pl.ds(2, 3), pl.ds(pl.multiple_of(8 + c * 16, 8), 16), CHUNKS + c)

    def edge(k):
        return cat_message(pl.ds(0, 5), pl.ds(248 * k, 8), 2 * CHUNKS + k)

    def lon_message(d, start, size, k):
        rows = pl.ds(start, size)
        return remote(XS.at[d, rows, :], XR.at[d, rows, :], lon_send.at[k, d], lon_recv.at[k, d], sides[d])

    def lon_chunk(d, c):
        return lon_message(d, pl.multiple_of(8 + c * 16, 8), 16, c)

    def lon_edge(d, k):
        return lon_message(d, 248 * k, 8, CHUNKS + k)

    def lon_static(d):
        return remote(LS.at[d], LR.at[d], edge_send.at[d], edge_recv.at[d], sides[d])

    def lat_message(d, k):
        fields = pl.ds(0, 9) if k == 0 else pl.ds(9, 3)
        here, there, device = ((FIRST + 1, LAST, up), (LAST - 1, FIRST, down))[d]
        return remote(
            F.at[fields, :, pl.ds(8 * here, 8), :], F.at[fields, :, pl.ds(8 * there, 8), :],
            lat_send.at[k, d], lat_recv.at[k, d], device,
        )

    def pack(first, count, send, row, size):
        iota = lane if size == 8 else lane16
        rows = pl.ds(row, size)
        from_rows = pl.ds(row + TOP_ROW, size)
        left = jnp.zeros((size, 128), jnp.float32)
        right = jnp.zeros((size, 128), jnp.float32)
        for i in range(count):
            mine = (iota >= 8 * i) & (iota < 8 * i + 8)
            a = F[first + i, 0, from_rows, :]
            b = F[first + i, 4, from_rows, :]
            left = jnp.where(mine, pltpu.roll(a, 8 * i, 1) if i else a, left)
            right = jnp.where(mine, pltpu.roll(b, 8 * i + 8, 1), right)
        send[0, rows, :] = left
        send[1, rows, :] = right

    def unpack(first, count, recv, row, size):
        iota = lane if size == 8 else lane16
        rows = pl.ds(row, size)
        a = recv[0, rows, :]
        b = recv[1, rows, :]
        for i in range(count):
            ahead = pltpu.roll(a, 128 - 8 * i, 1) if i else a
            behind = pltpu.roll(b, 120 - 8 * i, 1)
            F[first + i, 5, pl.ds(row + TOP_ROW, size), :] = jnp.where(
                iota < 8, ahead, jnp.where(iota >= 120, behind, 0.0)
            )

    def totals(places, row, size):
        for place in places:
            for f in range(3):
                F[ST + f, ORDER[place], pl.ds(row + TOP_ROW, size), :] = (
                    PT[f, place, pl.ds(row, size), :] + QT[f, place, pl.ds(row, size), :]
                )

    def right_less_left(before, here, after):
        ahead = pltpu.roll(jnp.where(lane == 0, after, here), 127, 1)
        behind = pltpu.roll(jnp.where(lane == 127, before, here), 1, 1)
        return ahead - behind

    def coefficients(band):
        rows = pl.ds(pl.multiple_of(8 * band, 8), 8)
        for j in range(6):
            wet = F[WT, j, rows, :]
            mass = F[MA, j, rows, :]
            cover = F[CO, j, rows, :]
            g = wet / (mass + F[DR, j, rows, :] + 1.0 - wet)
            push = g * cover
            F[MA, j, rows, :] = g * mass
            F[WX, j, rows, :] = push * F[WX, j, rows, :]
            F[WY, j, rows, :] = push * F[WY, j, rows, :]
            F[DR, j, rows, :] = 0.25 * g
            F[WT, j, rows, :] = wet * (1.0 / 3.0)

    def stress(band):
        row = pl.multiple_of(8 * band, 8)
        rows, above, below = pl.ds(row, 8), pl.ds(row - 1, 8), pl.ds(row + 1, 8)
        for j in range(6):
            before, after = (j + 5) % 6, (j + 1) % 6
            ux = right_less_left(F[U, before, rows, :], F[U, j, rows, :], F[U, after, rows, :])
            vx = right_less_left(F[V, before, rows, :], F[V, j, rows, :], F[V, after, rows, :])
            uy = F[U, j, below, :] - F[U, j, above, :]
            vy = F[V, j, below, :] - F[V, j, above, :]
            div, ten, shr = ux + vy, ux - vy, uy + vx
            square = 0.25 * (div * div + 0.25 * (ten * ten + shr * shr)) + 0.0025
            strength = F[ST, j, rows, :]
            half = strength * lax.rsqrt(square)
            eighth = 0.25 * half
            third = F[WT, j, rows, :]
            F[S1, j, rows, :] = third * (F[S1, j, rows, :] + half * div - 2.0 * strength)
            F[S2, j, rows, :] = third * (F[S2, j, rows, :] + eighth * ten)
            F[S12, j, rows, :] = third * (F[S12, j, rows, :] + eighth * shr)

    def momentum(band):
        row = pl.multiple_of(8 * band, 8)
        rows, above, below = pl.ds(row, 8), pl.ds(row - 1, 8), pl.ds(row + 1, 8)
        for j in range(6):
            around = ((j + 5) % 6, j, (j + 1) % 6)
            px = right_less_left(*(F[S1, k, rows, :] + F[S2, k, rows, :] for k in around))
            cx = right_less_left(*(F[S12, k, rows, :] for k in around))
            cy = F[S12, j, below, :] - F[S12, j, above, :]
            my = (F[S1, j, below, :] - F[S2, j, below, :]) - (F[S1, j, above, :] - F[S2, j, above, :])
            a, g = F[MA, j, rows, :], F[DR, j, rows, :]
            u, v = F[U, j, rows, :], F[V, j, rows, :]
            F[U, j, rows, :] = a * (u + 0.5 * v) + g * (px + 2.0 * cy) + F[WX, j, rows, :]
            F[V, j, rows, :] = a * (v - 0.5 * u) + g * (2.0 * cx + my) + F[WY, j, rows, :]

    def step(t):
        @pl.when(t <= LAST - FIRST)
        def _():
            coefficients(t + FIRST)
            stress(t + FIRST)

        for lag in range(1, 8):
            @pl.when((t >= lag) & (t <= LAST - FIRST + lag))
            def _():
                (momentum if lag % 2 else stress)(t + (FIRST - lag))

    def out_copies(row, size, k):
        return [
            pltpu.make_async_copy(
                F.at[pl.ds(0, 5), j, pl.ds(row + TOP_ROW, size), :],
                out.at[:, pl.ds(row, size), pl.ds(j * 128, 128)],
                out_sem.at[k, j],
            )
            for j in range(TILES)
        ]

    for i, block in ((0, 0), (1, 15)):
        for copy in load(i):
            copy.wait()
        sums(block, 0)
    pl.semaphore_wait(barrier, 5)
    edge(0).start()
    edge(1).start()
    for copy in load(2):
        copy.wait()
    lax.fori_loop(1, 4, sums, 0)
    border(0).start()
    border(1).start()
    inner(0).start()
    border(2).start()
    inner(1).start()

    for copy in field_loads():
        copy.wait()

    def given(block, carry):
        row = pl.multiple_of(block * 16, 16)
        for j in range(TILES):
            F[WT, j, pl.ds(row + TOP_ROW, 16), :] = LAND[pl.ds(row, 16), pl.ds(j * 128, 128)].astype(jnp.float32)
        pack(0, 9, LS, row, 16)
        return carry

    lax.fori_loop(0, 16, given, 0)
    for d in range(2):
        lon_static(d).start()

    for copy in load(3):
        copy.wait()
    lax.fori_loop(4, 8, sums, 0)
    border(3).start()
    inner(2).start()

    for k in range(2):
        edge(k).wait_recv()
        totals(range(5), 248 * k, 8)
        pack(ST, 3, XS, 248 * k, 8)
        for d in range(2):
            lon_edge(d, k).start()
    for i in (4, 5):
        for copy in load(i):
            copy.wait()
    lax.fori_loop(8, 15, sums, 0)

    for d in range(2):
        lon_static(d).wait_recv()

    def take(block, carry):
        unpack(0, 9, LR, pl.multiple_of(block * 16, 16), 16)
        return carry

    lax.fori_loop(0, 16, take, 0)
    for k in range(2):
        for d in range(2):
            lon_edge(d, k).wait_recv()
        unpack(ST, 3, XR, 248 * k, 8)

    @pl.when(has_up)
    def _():
        lat_message(0, 0).start()
        lat_message(0, 1).start()

    @pl.when(has_down)
    def _():
        lat_message(1, 0).start()
        lat_message(1, 1).start()

    for c in range(4, AHEAD + 1):
        border(c).start()
        inner(c - 1).start()

    def columns(c):
        row = pl.multiple_of(8 + c * 16, 8)
        border(c).wait_recv()
        totals(range(2), row, 16)
        pack(ST, 3, XS, row, 16)
        for d in range(2):
            lon_chunk(d, c).start()

    columns(0)

    @pl.when(has_down)
    def _():
        lat_message(0, 0).wait_recv()
        lat_message(0, 1).wait_recv()

    @pl.when(has_up)
    def _():
        lat_message(1, 0).wait_recv()
        lat_message(1, 1).wait_recv()

    @pl.when(has_up)
    def _():
        lat_message(0, 0).wait_send()
        lat_message(0, 1).wait_send()

    @pl.when(has_down)
    def _():
        lat_message(1, 0).wait_send()
        lat_message(1, 1).wait_send()

    def early(t, carry):
        step(t)
        return carry

    lax.fori_loop(0, 2, early, 0)

    def chunk(c, carry):
        @pl.when(c < CHUNKS - 1)
        def _():
            columns(c + 1)

        row = pl.multiple_of(8 + c * 16, 8)
        for d in range(2):
            lon_chunk(d, c).wait_recv()
        unpack(ST, 3, XR, row, 16)
        inner(c).wait_recv()

        @pl.when(c + AHEAD + 1 < CHUNKS)
        def _():
            border(c + AHEAD + 1).start()

        @pl.when(c + AHEAD < CHUNKS)
        def _():
            inner(c + AHEAD).start()

        totals(range(2, 5), row, 16)
        lax.fori_loop(2 * c + 2, 2 * c + 4, early, 0)

        @pl.when(c >= 3)
        def _():
            for copy in out_copies(pl.multiple_of((c - 3) * 16, 16), 16, c - 3):
                copy.start()

        return carry

    lax.fori_loop(0, CHUNKS, chunk, 0)
    lax.fori_loop(32, 40, early, 0)
    last = CHUNKS - 3
    for copy in out_copies(last * 16, ROWS - last * 16, last):
        copy.start()

    def finish(c, carry):
        border(c).wait_send()
        inner(c).wait_send()
        for d in range(2):
            lon_chunk(d, c).wait_send()

        @pl.when(c < last)
        def _():
            for copy in out_copies(pl.multiple_of(c * 16, 16), 16, c):
                copy.wait()

        return carry

    lax.fori_loop(0, CHUNKS, finish, 0)
    for k in range(2):
        edge(k).wait_send()
        lon_static(k).wait_send()
        for d in range(2):
            lon_edge(d, k).wait_send()
    for copy in out_copies(last * 16, ROWS - last * 16, last):
        copy.wait()


def shards(*arrays):
    dma = pltpu.SemaphoreType.DMA
    f32 = jnp.float32
    hbm = pl.BlockSpec(memory_space=pl.ANY)
    specs = [hbm] * len(arrays)
    specs[2] = pl.BlockSpec(memory_space=pltpu.SMEM)
    result = pl.pallas_call(
        kernel,
        out_shape=jax.ShapeDtypeStruct((5, ROWS, COLS), f32),
        in_specs=specs,
        out_specs=pl.BlockSpec(memory_space=pl.ANY),
        scratch_shapes=[
            pltpu.VMEM((12, 6, HEIGHT, 128), f32),
            pltpu.VMEM((NCAT, ROWS, COLS), jnp.bfloat16),
            pltpu.VMEM((NCAT, ROWS, COLS), jnp.bfloat16),
            pltpu.VMEM((ROWS, COLS), jnp.int32),
            pltpu.VMEM((ROWS, COLS), jnp.int32),
            pltpu.VMEM((3, TILES, ROWS, 128), f32),
            pltpu.VMEM((3, TILES, ROWS, 128), f32),
            pltpu.VMEM((2, ROWS, 128), f32),
            pltpu.VMEM((2, ROWS, 128), f32),
            pltpu.VMEM((2, ROWS, 128), f32),
            pltpu.VMEM((2, ROWS, 128), f32),
            dma((2 * CHUNKS + 2,)),
            dma((2 * CHUNKS + 2,)),
            dma((CHUNKS + 2, 2)),
            dma((CHUNKS + 2, 2)),
            dma((2,)),
            dma((2,)),
            dma((2, 2)),
            dma((2, 2)),
            dma((len(LOADS), 3)),
            dma((9, TILES)),
            dma((CHUNKS, TILES)),
        ],
        compiler_params=pltpu.CompilerParams(
            collective_id=0, has_side_effects=True, vmem_limit_bytes=60 * 2**20 + 2**18
        ),
        name="ice",
    )(*arrays)
    return tuple(result[i] for i in range(5))


def solution(mesh):
    block = P("cat", "lat", "lon")
    plane = P("lat", "lon")
    return jax.shard_map(
        shards,
        mesh=mesh,
        in_specs=(block, block, P("cat"), *[plane] * 10),
        out_specs=(plane,) * 5,
        check_vma=False,
    )
```

time: 159 us -> 84.3 us (0.53)
  the two profiles are of different devices: /device:TPU:1 before, /device:TPU:6 now
where the time goes in v1:
time: 84.3 us; the launch traced here: 84.2 us
  Pallas kernels  79.9 us (95%)
  local copies, waits for them, and re-layouts  3.62 us (4%)
    pallas_call x1, Pallas kernels, shards(): pl.pallas_call(kernel, out_shape=jax.ShapeDtypeStruct((5, ROWS, COLS), f3...  79.9 us
    squeeze x1, local copies, waits for them, and re-layouts, shards(): return tuple((result[i] for i in range(5)))  3.62 us

profile of v1, /device:TPU:6, one launch (start us, length us, event | category | flops | bytes accessed | tf_op | source)
XLA Modules:
  0.0 84.2 jit_solution(17169441683401005340)
XLA Ops:
  0.6 79.9 %ice.1 = f32[5,256,640]{2,1,0:T(8,128)} custom-call(bf16[20,256,640]{2,1,0:T(8,128)(2,1)} %th.1, bf16[20,256,640]{2,1,0:T(8,128)(2,1)} %ar.1, f32[20]{0:T(128)} %weight.1, s32[256,640]{1,0:T(8,128)} %top.1, s32[256,640]{1,0:T(8,128)} %land.1, f32[256,640]{1,0:T(8,128)} %u0.1, f32[256,640]{1,0:T(8,128)} %v0.1, f32[256,640]{1,0:T(8,128)} %d0.1, ...), custom_call_target="tpu_custom_call" | custom-call | tf_op jit(solution)/shard_map/ice/pallas_call | solution.py:425
  80.6 3.6 %slice_bitcast_fusion = (f32[256,640]{1,0:T(8,128)}, f32[256,640]{1,0:T(8,128)}, f32[256,640]{1,0:T(8,128)}, f32[256,640]{1,0:T(8,128)}, f32[256,640]{1,0:T(8,128)}) fusion(f32[5,256,640]{2,1,0:T(8,128)} %ice.1), kind=kLoop, calls=%fused_computation | loop fusion | bytes 6553600 | tf_op jit(solution)/shard_map/squeeze | solution.py:459

commit v2 on v1

--- a/solution.py
+++ b/solution.py
@@ -11,7 +11,9 @@
 COLS = 640
 TILES = 5
 CHUNKS = 15
-AHEAD = 5
+COLUMNS_AHEAD = 3
+BORDERS_AHEAD = 8
+INNERS_AHEAD = 6
 ORDER = (0, 4, 1, 2, 3)
 TOP_ROW = 72
 HEIGHT = 344
@@ -21,19 +23,15 @@
 
 
 def kernel(th, ar, weight, top, land, u0, v0, d0, t0, h0, wx0, wy0, dr0, out,
-           F, T, A, TOP, LAND, PT, QT, LS, LR, XS, XR,
+           F, W, T, A, TOP, LAND, PT, QT, LS, LR, XS, XR,
            cat_send, cat_recv, lon_send, lon_recv, edge_send, edge_recv, lat_send, lat_recv,
-           load_sem, field_sem, out_sem):
+           load_sem, field_sem):
     cat, lat, lon = lax.axis_index("cat"), lax.axis_index("lat"), lax.axis_index("lon")
     peer = (1 - cat, lat, lon)
     sides = ((cat, lat, lax.rem(lon + 15, 16)), (cat, lat, lax.rem(lon + 1, 16)))
     up = (cat, lax.rem(lat + 3, 4), lon)
     down = (cat, lax.rem(lat + 1, 4), lon)
     has_up, has_down = lat > 0, lat < 3
-
-    barrier = pltpu.get_barrier_semaphore()
-    for device in (peer, *sides, up, down):
-        pl.semaphore_signal(barrier, inc=1, device_id=device, device_id_type=MESH)
 
     def load(i):
         start, size = LOADS[i]
@@ -55,19 +53,16 @@
                 )
         return copies
 
-    for i in range(3):
+    weights = pltpu.make_async_copy(weight, W, field_sem.at[8, 1])
+    for i in range(2):
         for copy in load(i):
             copy.start()
-    for copy in field_loads():
+    weights.start()
+    barrier = pltpu.get_barrier_semaphore()
+    for device in (peer, *sides, up, down):
+        pl.semaphore_signal(barrier, inc=1, device_id=device, device_id_type=MESH)
+    for copy in load(2):
         copy.start()
-    for i in range(3, len(LOADS)):
-        for copy in load(i):
-            copy.start()
-
-    for f in range(5):
-        for j in range(6):
-            F[f, j, pl.ds(8 * FIRST - 8, 8), :] = jnp.zeros((8, 128), jnp.float32)
-            F[f, j, pl.ds(8 * LAST + 8, 8), :] = jnp.zeros((8, 128), jnp.float32)
 
     @pl.when(lat == 0)
     def _():
@@ -96,7 +91,7 @@
                 m = c * h
                 cover = cover + c
                 mass = mass + m
-                strength = strength + (weight[n] * h) * m
+                strength = strength + (W[n] * h) * m
             PT[0, place, rows, :] = strength
             PT[1, place, rows, :] = mass
             PT[2, place, rows, :] = cover
@@ -134,10 +129,12 @@
         return remote(LS.at[d], LR.at[d], edge_send.at[d], edge_recv.at[d], sides[d])
 
     def lat_message(d, k):
-        fields = pl.ds(0, 9) if k == 0 else pl.ds(9, 3)
+        fields, tiles = (
+            (pl.ds(0, 9), pl.ds(0, TILES)), (pl.ds(9, 3), pl.ds(0, TILES)), (pl.ds(0, 12), pl.ds(TILES, 1))
+        )[k]
         here, there, device = ((FIRST + 1, LAST, up), (LAST - 1, FIRST, down))[d]
         return remote(
-            F.at[fields, :, pl.ds(8 * here, 8), :], F.at[fields, :, pl.ds(8 * there, 8), :],
+            F.at[fields, tiles, pl.ds(8 * here, 8), :], F.at[fields, tiles, pl.ds(8 * there, 8), :],
             lat_send.at[k, d], lat_recv.at[k, d], device,
         )
 
@@ -194,7 +191,7 @@
             F[DR, j, rows, :] = 0.25 * g
             F[WT, j, rows, :] = wet * (1.0 / 3.0)
 
-    def stress(band):
+    def stress(band, last=None):
         row = pl.multiple_of(8 * band, 8)
         rows, above, below = pl.ds(row, 8), pl.ds(row - 1, 8), pl.ds(row + 1, 8)
         for j in range(6):
@@ -209,11 +206,19 @@
             half = strength * lax.rsqrt(square)
             eighth = 0.25 * half
             third = F[WT, j, rows, :]
-            F[S1, j, rows, :] = third * (F[S1, j, rows, :] + half * div - 2.0 * strength)
-            F[S2, j, rows, :] = third * (F[S2, j, rows, :] + eighth * ten)
-            F[S12, j, rows, :] = third * (F[S12, j, rows, :] + eighth * shr)
-
-    def momentum(band):
+            s1 = third * (F[S1, j, rows, :] + half * div - 2.0 * strength)
+            s2 = third * (F[S2, j, rows, :] + eighth * ten)
+            s12 = third * (F[S12, j, rows, :] + eighth * shr)
+            F[S1, j, rows, :] = s1
+            F[S2, j, rows, :] = s2
+            F[S12, j, rows, :] = s12
+            if last is not None and j < TILES:
+                place = (pl.ds(last, 8), pl.ds(j * 128, 128))
+                out[(S1, *place)] = s1
+                out[(S2, *place)] = s2
+                out[(S12, *place)] = s12
+
+    def momentum(band, last=None):
         row = pl.multiple_of(8 * band, 8)
         rows, above, below = pl.ds(row, 8), pl.ds(row - 1, 8), pl.ds(row + 1, 8)
         for j in range(6):
@@ -224,45 +229,51 @@
             my = (F[S1, j, below, :] - F[S2, j, below, :]) - (F[S1, j, above, :] - F[S2, j, above, :])
             a, g = F[MA, j, rows, :], F[DR, j, rows, :]
             u, v = F[U, j, rows, :], F[V, j, rows, :]
-            F[U, j, rows, :] = a * (u + 0.5 * v) + g * (px + 2.0 * cy) + F[WX, j, rows, :]
-            F[V, j, rows, :] = a * (v - 0.5 * u) + g * (2.0 * cx + my) + F[WY, j, rows, :]
-
-    def step(t):
-        @pl.when(t <= LAST - FIRST)
-        def _():
-            coefficients(t + FIRST)
-            stress(t + FIRST)
-
-        for lag in range(1, 8):
-            @pl.when((t >= lag) & (t <= LAST - FIRST + lag))
-            def _():
-                (momentum if lag % 2 else stress)(t + (FIRST - lag))
-
-    def out_copies(row, size, k):
-        return [
-            pltpu.make_async_copy(
-                F.at[pl.ds(0, 5), j, pl.ds(row + TOP_ROW, size), :],
-                out.at[:, pl.ds(row, size), pl.ds(j * 128, 128)],
-                out_sem.at[k, j],
-            )
-            for j in range(TILES)
-        ]
-
+            next_u = a * (u + 0.5 * v) + g * (px + 2.0 * cy) + F[WX, j, rows, :]
+            next_v = a * (v - 0.5 * u) + g * (2.0 * cx + my) + F[WY, j, rows, :]
+            if last is None:
+                F[U, j, rows, :] = next_u
+                F[V, j, rows, :] = next_v
+            elif j < TILES:
+                place = (pl.ds(last, 8), pl.ds(j * 128, 128))
+                out[(U, *place)] = next_u
+                out[(V, *place)] = next_v
+
+    def half_stage(lag, band):
+        last = None
+        if lag >= 6:
+            row = 8 * (band - FIRST - 1)
+            last = max(row, 0) if isinstance(band, int) else pl.multiple_of(jnp.maximum(row, 0), 8)
+            if isinstance(band, int) and band == LAST:
+                last = None
+        (momentum if lag % 2 else stress)(band, last)
+
+    def step(t, carry):
+        coefficients(t + FIRST)
+        for lag in range(8):
+            half_stage(lag, t + (FIRST - lag))
+        return carry
+
+    weights.wait()
     for i, block in ((0, 0), (1, 15)):
         for copy in load(i):
             copy.wait()
+        if i == 1:
+            for copy in field_loads():
+                copy.start()
+            for late in range(3, len(LOADS)):
+                for copy in load(late):
+                    copy.start()
         sums(block, 0)
-    pl.semaphore_wait(barrier, 5)
-    edge(0).start()
-    edge(1).start()
+        if i == 0:
+            pl.semaphore_wait(barrier, 5)
+        edge(i).start()
     for copy in load(2):
         copy.wait()
     lax.fori_loop(1, 4, sums, 0)
-    border(0).start()
-    border(1).start()
+    for c in range(3):
+        border(c).start()
     inner(0).start()
-    border(2).start()
-    inner(1).start()
 
     for copy in field_loads():
         copy.wait()
@@ -278,11 +289,22 @@
     for d in range(2):
         lon_static(d).start()
 
+    def to_rows(k):
+        @pl.when(has_up)
+        def _():
+            lat_message(0, k).start()
+
+        @pl.when(has_down)
+        def _():
+            lat_message(1, k).start()
+
+    to_rows(0)
     for copy in load(3):
         copy.wait()
     lax.fori_loop(4, 8, sums, 0)
     border(3).start()
-    inner(2).start()
+    inner(1).start()
+    border(4).start()
 
     for k in range(2):
         edge(k).wait_recv()
@@ -290,6 +312,7 @@
         pack(ST, 3, XS, 248 * k, 8)
         for d in range(2):
             lon_edge(d, k).start()
+    to_rows(1)
     for i in (4, 5):
         for copy in load(i):
             copy.wait()
@@ -307,20 +330,11 @@
         for d in range(2):
             lon_edge(d, k).wait_recv()
         unpack(ST, 3, XR, 248 * k, 8)
-
-    @pl.when(has_up)
-    def _():
-        lat_message(0, 0).start()
-        lat_message(0, 1).start()
-
-    @pl.when(has_down)
-    def _():
-        lat_message(1, 0).start()
-        lat_message(1, 1).start()
-
-    for c in range(4, AHEAD + 1):
+    to_rows(2)
+    for c in range(5, BORDERS_AHEAD):
+        inner(c - 3).start()
         border(c).start()
-        inner(c - 1).start()
+    inner(BORDERS_AHEAD - 3).start()
 
     def columns(c):
         row = pl.multiple_of(8 + c * 16, 8)
@@ -330,38 +344,27 @@
         for d in range(2):
             lon_chunk(d, c).start()
 
-    columns(0)
+    for c in range(COLUMNS_AHEAD):
+        columns(c)
 
     @pl.when(has_down)
     def _():
-        lat_message(0, 0).wait_recv()
-        lat_message(0, 1).wait_recv()
+        for k in range(3):
+            lat_message(0, k).wait_recv()
+            lat_message(1, k).wait_send()
 
     @pl.when(has_up)
     def _():
-        lat_message(1, 0).wait_recv()
-        lat_message(1, 1).wait_recv()
-
-    @pl.when(has_up)
-    def _():
-        lat_message(0, 0).wait_send()
-        lat_message(0, 1).wait_send()
-
-    @pl.when(has_down)
-    def _():
-        lat_message(1, 0).wait_send()
-        lat_message(1, 1).wait_send()
-
-    def early(t, carry):
-        step(t)
-        return carry
-
-    lax.fori_loop(0, 2, early, 0)
+        for k in range(3):
+            lat_message(1, k).wait_recv()
+            lat_message(0, k).wait_send()
+
+    lax.fori_loop(0, 2, step, 0)
 
     def chunk(c, carry):
-        @pl.when(c < CHUNKS - 1)
+        @pl.when(c + COLUMNS_AHEAD < CHUNKS)
         def _():
-            columns(c + 1)
+            columns(c + COLUMNS_AHEAD)
 
         row = pl.multiple_of(8 + c * 16, 8)
         for d in range(2):
@@ -369,41 +372,29 @@
         unpack(ST, 3, XR, row, 16)
         inner(c).wait_recv()
 
-        @pl.when(c + AHEAD + 1 < CHUNKS)
+        @pl.when(c + BORDERS_AHEAD < CHUNKS)
         def _():
-            border(c + AHEAD + 1).start()
-
-        @pl.when(c + AHEAD < CHUNKS)
+            border(c + BORDERS_AHEAD).start()
+
+        @pl.when(c + INNERS_AHEAD < CHUNKS)
         def _():
-            inner(c + AHEAD).start()
+            inner(c + INNERS_AHEAD).start()
 
         totals(range(2, 5), row, 16)
-        lax.fori_loop(2 * c + 2, 2 * c + 4, early, 0)
-
-        @pl.when(c >= 3)
-        def _():
-            for copy in out_copies(pl.multiple_of((c - 3) * 16, 16), 16, c - 3):
-                copy.start()
-
+        lax.fori_loop(2 * c + 2, 2 * c + 4, step, 0)
         return carry
 
     lax.fori_loop(0, CHUNKS, chunk, 0)
-    lax.fori_loop(32, 40, early, 0)
-    last = CHUNKS - 3
-    for copy in out_copies(last * 16, ROWS - last * 16, last):
-        copy.start()
+    lax.fori_loop(32, 34, step, 0)
+    for t in range(34, 40):
+        for lag in range(t - 33, 8):
+            half_stage(lag, t + FIRST - lag)
 
     def finish(c, carry):
         border(c).wait_send()
         inner(c).wait_send()
         for d in range(2):
             lon_chunk(d, c).wait_send()
-
-        @pl.when(c < last)
-        def _():
-            for copy in out_copies(pl.multiple_of(c * 16, 16), 16, c):
-                copy.wait()
-
         return carry
 
     lax.fori_loop(0, CHUNKS, finish, 0)
@@ -412,23 +403,19 @@
         lon_static(k).wait_send()
         for d in range(2):
             lon_edge(d, k).wait_send()
-    for copy in out_copies(last * 16, ROWS - last * 16, last):
-        copy.wait()
 
 
 def shards(*arrays):
     dma = pltpu.SemaphoreType.DMA
     f32 = jnp.float32
-    hbm = pl.BlockSpec(memory_space=pl.ANY)
-    specs = [hbm] * len(arrays)
-    specs[2] = pl.BlockSpec(memory_space=pltpu.SMEM)
     result = pl.pallas_call(
         kernel,
         out_shape=jax.ShapeDtypeStruct((5, ROWS, COLS), f32),
-        in_specs=specs,
-        out_specs=pl.BlockSpec(memory_space=pl.ANY),
+        in_specs=[pl.BlockSpec(memory_space=pltpu.HBM)] * len(arrays),
+        out_specs=pl.BlockSpec(memory_space=pltpu.VMEM),
         scratch_shapes=[
             pltpu.VMEM((12, 6, HEIGHT, 128), f32),
+            pltpu.SMEM((NCAT,), f32),
             pltpu.VMEM((NCAT, ROWS, COLS), jnp.bfloat16),
             pltpu.VMEM((NCAT, ROWS, COLS), jnp.bfloat16),
             pltpu.VMEM((ROWS, COLS), jnp.int32),
@@ -445,17 +432,16 @@
             dma((CHUNKS + 2, 2)),
             dma((2,)),
             dma((2,)),
-            dma((2, 2)),
-            dma((2, 2)),
+            dma((3, 2)),
+            dma((3, 2)),
             dma((len(LOADS), 3)),
             dma((9, TILES)),
-            dma((CHUNKS, TILES)),
         ],
         compiler_params=pltpu.CompilerParams(
-            collective_id=0, has_side_effects=True, vmem_limit_bytes=60 * 2**20 + 2**18
+            collective_id=0, has_side_effects=True, vmem_limit_bytes=44 * 2**20
         ),
         name="ice",
-    )(*arrays)
+    )(*(pltpu.with_memory_space_constraint(a, pltpu.HBM) for a in arrays))
     return tuple(result[i] for i in range(5))
 
 

time: 84.3 us -> 63.7 us (0.76)
  the two profiles are of different devices: /device:TPU:6 before, /device:TPU:2 now
where the time goes in v2:
time: 63.7 us; the launch traced here: 63.5 us
  Pallas kernels  61.2 us (96%)
  local copies, waits for them, and re-layouts  1.74 us (3%)
  between operations  0.64 us (1%)
    pallas_call x1, Pallas kernels, shards(): pl.pallas_call(kernel, out_shape=jax.ShapeDtypeStruct((5, ROWS, COLS), f3...  61.2 us
    squeeze x1, local copies, waits for them, and re-layouts, shards(): return tuple((result[i] for i in range(5)))  1.74 us

profile of v2, /device:TPU:2, one launch (start us, length us, event | category | flops | bytes accessed | tf_op | source)
XLA Modules:
  0.0 63.5 jit_solution(8157630072341578095)
XLA Ops:
  0.6 61.2 %ice.1 = f32[5,256,640]{2,1,0:T(8,128)S(1)} custom-call(bf16[20,256,640]{2,1,0:T(8,128)(2,1)} %th.1, bf16[20,256,640]{2,1,0:T(8,128)(2,1)} %ar.1, f32[20]{0:T(128)} %weight.1, s32[256,640]{1,0:T(8,128)} %top.1, s32[256,640]{1,0:T(8,128)} %land.1, f32[256,640]{1,0:T(8,128)} %u0.1, f32[256,640]{1,0:T(8,128)} %v0.1, f32[256,640]{1,0:T(8,128)} %d0.1, ...), custom_call_target="tpu_custom_call" | custom-call | tf_op jit(solution)/shard_map/ice/pallas_call | solution.py:411
  61.8 1.7 %slice_bitcast_fusion = (f32[256,640]{1,0:T(8,128)}, f32[256,640]{1,0:T(8,128)}, f32[256,640]{1,0:T(8,128)}, f32[256,640]{1,0:T(8,128)}, f32[256,640]{1,0:T(8,128)}) fusion(f32[5,256,640]{2,1,0:T(8,128)S(1)} %ice.1), kind=kLoop, calls=%fused_computation | loop fusion | bytes 6553600 | tf_op jit(solution)/shard_map/squeeze | solution.py:445

commit v3 on v2

--- a/solution.py
+++ b/solution.py
@@ -11,21 +11,22 @@
 COLS = 640
 TILES = 5
 CHUNKS = 15
-COLUMNS_AHEAD = 3
-BORDERS_AHEAD = 8
+COLUMNS_AHEAD = 6
+BORDERS_AHEAD = 12
 INNERS_AHEAD = 6
 ORDER = (0, 4, 1, 2, 3)
 TOP_ROW = 72
 HEIGHT = 344
 FIRST, LAST = 8, 41
 LOADS = ((0, 16), (240, 16), (16, 48), (64, 64), (128, 64), (192, 48))
+TOPS = ((0, 16), (240, 16), (16, 224))
 MESH = pl.DeviceIdType.MESH
 
 
 def kernel(th, ar, weight, top, land, u0, v0, d0, t0, h0, wx0, wy0, dr0, out,
-           F, W, T, A, TOP, LAND, PT, QT, LS, LR, XS, XR,
+           F, W, TA, TOP, LAND, PT, QT, LS, LR, XS, XR,
            cat_send, cat_recv, lon_send, lon_recv, edge_send, edge_recv, lat_send, lat_recv,
-           load_sem, field_sem):
+           load_sem, top_sem, field_sem, near):
     cat, lat, lon = lax.axis_index("cat"), lax.axis_index("lat"), lax.axis_index("lon")
     peer = (1 - cat, lat, lon)
     sides = ((cat, lat, lax.rem(lon + 15, 16)), (cat, lat, lax.rem(lon + 1, 16)))
@@ -33,36 +34,67 @@
     down = (cat, lax.rem(lat + 1, 4), lon)
     has_up, has_down = lat > 0, lat < 3
 
-    def load(i):
-        start, size = LOADS[i]
-        rows = pl.ds(start, size)
-        return (
-            pltpu.make_async_copy(top.at[rows, :], TOP.at[rows, :], load_sem.at[i, 0]),
-            pltpu.make_async_copy(th.at[:, rows, :], T.at[:, rows, :], load_sem.at[i, 1]),
-            pltpu.make_async_copy(ar.at[:, rows, :], A.at[:, rows, :], load_sem.at[i, 2]),
-        )
-
-    def field_loads():
-        copies = [pltpu.make_async_copy(land, LAND, field_sem.at[8, 0])]
+    even = lax.rem(lon, 2) == 0
+
+    def load_rows(i):
+        return pl.ds(*LOADS[i])
+
+    def start_load(i):
+        rows = load_rows(i)
+        if i < len(TOPS):
+            some = pl.ds(*TOPS[i])
+            pltpu.make_async_copy(top.at[some, :], TOP.at[some, :], top_sem.at[i]).start()
+        for k, ref in enumerate((th, ar)):
+            pltpu.make_async_copy(ref.at[:, rows, :], TA.at[k, :, rows, :], load_sem.at[i]).start()
+
+    def wait_load(i):
+        if i < len(TOPS):
+            some = TOP.at[pl.ds(*TOPS[i]), :]
+            pltpu.make_async_copy(some, some, top_sem.at[i]).wait()
+        both = TA.at[:, :, load_rows(i), :]
+        pltpu.make_async_copy(both, both, load_sem.at[i]).wait()
+
+    lands = pltpu.make_async_copy(land, LAND, field_sem.at[1])
+    weights = pltpu.make_async_copy(weight, W, field_sem.at[2])
+
+    def start_fields():
         for f, ref in enumerate((u0, v0, d0, t0, h0, wx0, wy0, dr0)):
             for j in range(TILES):
-                copies.append(
-                    pltpu.make_async_copy(
-                        ref.at[:, pl.ds(j * 128, 128)], F.at[f, j, pl.ds(TOP_ROW, ROWS), :], field_sem.at[f, j]
-                    )
-                )
-        return copies
-
-    weights = pltpu.make_async_copy(weight, W, field_sem.at[8, 1])
-    for i in range(2):
-        for copy in load(i):
-            copy.start()
+                pltpu.make_async_copy(
+                    ref.at[:, pl.ds(j * 128, 128)], F.at[f, j, pl.ds(TOP_ROW, ROWS), :], field_sem.at[0]
+                ).start()
+        lands.start()
+
+    def wait_fields():
+        given = F.at[pl.ds(0, 8), pl.ds(0, TILES), pl.ds(TOP_ROW, ROWS), :]
+        pltpu.make_async_copy(given, given, field_sem.at[0]).wait()
+        lands.wait()
+
+    start_load(0)
     weights.start()
+    start_load(1)
     barrier = pltpu.get_barrier_semaphore()
-    for device in (peer, *sides, up, down):
+    for device in (peer, up, down):
         pl.semaphore_signal(barrier, inc=1, device_id=device, device_id_type=MESH)
-    for copy in load(2):
-        copy.start()
+
+    @pl.when(even)
+    def _():
+        for device in sides:
+            pl.semaphore_signal(barrier, inc=1, device_id=device, device_id_type=MESH)
+
+    def enter():
+        @pl.when(even)
+        def _():
+            pl.semaphore_wait(barrier, 3)
+
+        @pl.when(jnp.logical_not(even))
+        def _():
+            pl.semaphore_wait(barrier, 5)
+            for device in sides:
+                pl.semaphore_signal(near, inc=1, device_id=device, device_id_type=MESH)
+
+    start_load(2)
+    start_load(3)
 
     @pl.when(lat == 0)
     def _():
@@ -85,8 +117,8 @@
             mass = jnp.zeros((16, 128), jnp.float32)
             cover = jnp.zeros((16, 128), jnp.float32)
             for n in range(NCAT):
-                h = T[n, rows, cols].astype(jnp.float32)
-                c = A[n, rows, cols].astype(jnp.float32)
+                h = TA[0, n, rows, cols].astype(jnp.float32)
+                c = TA[1, n, rows, cols].astype(jnp.float32)
                 c = jnp.where(limit > n, c, 0.0)
                 m = c * h
                 cover = cover + c
@@ -104,7 +136,7 @@
 
     def cat_message(tiles, rows, k):
         where = (slice(None), tiles, rows, slice(None))
-        return remote(PT.at[where], QT.at[where], cat_send.at[k], cat_recv.at[k], peer)
+        return remote(PT.at[where], QT.at[where], cat_send, cat_recv.at[k], peer)
 
     def border(c):
         return cat_message(pl.ds(0, 2), pl.ds(pl.multiple_of(8 + c * 16, 8), 16), c)
@@ -112,30 +144,32 @@
     def inner(c):
         return cat_message(pl.ds(2, 3), pl.ds(pl.multiple_of(8 + c * 16, 8), 16), CHUNKS + c)
 
+    def last_inner(k):
+        return cat_message(pl.ds(2, 3), pl.ds(ROWS - 24 + 8 * k, 8), 2 * CHUNKS - 1 + k)
+
     def edge(k):
-        return cat_message(pl.ds(0, 5), pl.ds(248 * k, 8), 2 * CHUNKS + k)
-
-    def lon_message(d, start, size, k):
+        return cat_message(pl.ds(0, 5), pl.ds(248 * k, 8), 2 * CHUNKS + 1 + k)
+
+    def start_columns(start, size, k):
         rows = pl.ds(start, size)
-        return remote(XS.at[d, rows, :], XR.at[d, rows, :], lon_send.at[k, d], lon_recv.at[k, d], sides[d])
-
-    def lon_chunk(d, c):
-        return lon_message(d, pl.multiple_of(8 + c * 16, 8), 16, c)
-
-    def lon_edge(d, k):
-        return lon_message(d, 248 * k, 8, CHUNKS + k)
-
-    def lon_static(d):
-        return remote(LS.at[d], LR.at[d], edge_send.at[d], edge_recv.at[d], sides[d])
+        for d in range(2):
+            remote(XS.at[d, rows, :], XR.at[d, rows, :], lon_send, lon_recv.at[k], sides[d]).start()
+
+    def wait_columns(start, size, k):
+        rows = pl.ds(start, size)
+        remote(XS.at[:, rows, :], XR.at[:, rows, :], lon_send, lon_recv.at[k], sides[0]).wait_recv()
 
     def lat_message(d, k):
         fields, tiles = (
             (pl.ds(0, 9), pl.ds(0, TILES)), (pl.ds(9, 3), pl.ds(0, TILES)), (pl.ds(0, 12), pl.ds(TILES, 1))
         )[k]
+        return lat_copy(d, fields, tiles)
+
+    def lat_copy(d, fields, tiles):
         here, there, device = ((FIRST + 1, LAST, up), (LAST - 1, FIRST, down))[d]
         return remote(
             F.at[fields, tiles, pl.ds(8 * here, 8), :], F.at[fields, tiles, pl.ds(8 * there, 8), :],
-            lat_send.at[k, d], lat_recv.at[k, d], device,
+            lat_send.at[d], lat_recv.at[d], device,
         )
 
     def pack(first, count, send, row, size):
@@ -255,28 +289,27 @@
         return carry
 
     weights.wait()
-    for i, block in ((0, 0), (1, 15)):
-        for copy in load(i):
-            copy.wait()
-        if i == 1:
-            for copy in field_loads():
-                copy.start()
-            for late in range(3, len(LOADS)):
-                for copy in load(late):
-                    copy.start()
-        sums(block, 0)
-        if i == 0:
-            pl.semaphore_wait(barrier, 5)
-        edge(i).start()
-    for copy in load(2):
-        copy.wait()
+    wait_load(0)
+    sums(0, 0)
+    enter()
+    edge(0).start()
+    start_fields()
+    start_load(4)
+    start_load(5)
+    wait_load(1)
+    sums(15, 0)
+    edge(1).start()
+    wait_load(2)
     lax.fori_loop(1, 4, sums, 0)
     for c in range(3):
         border(c).start()
     inner(0).start()
-
-    for copy in field_loads():
-        copy.wait()
+    wait_load(3)
+    lax.fori_loop(4, 8, sums, 0)
+    border(3).start()
+    border(4).start()
+
+    wait_fields()
 
     def given(block, carry):
         row = pl.multiple_of(block * 16, 16)
@@ -286,8 +319,13 @@
         return carry
 
     lax.fori_loop(0, 16, given, 0)
+
+    @pl.when(even)
+    def _():
+        pl.semaphore_wait(near, 2)
+
     for d in range(2):
-        lon_static(d).start()
+        remote(LS.at[d], LR.at[d], edge_send, edge_recv, sides[d]).start()
 
     def to_rows(k):
         @pl.when(has_up)
@@ -299,27 +337,20 @@
             lat_message(1, k).start()
 
     to_rows(0)
-    for copy in load(3):
-        copy.wait()
-    lax.fori_loop(4, 8, sums, 0)
-    border(3).start()
-    inner(1).start()
-    border(4).start()
 
     for k in range(2):
         edge(k).wait_recv()
         totals(range(5), 248 * k, 8)
         pack(ST, 3, XS, 248 * k, 8)
-        for d in range(2):
-            lon_edge(d, k).start()
+        start_columns(248 * k, 8, CHUNKS + k)
     to_rows(1)
-    for i in (4, 5):
-        for copy in load(i):
-            copy.wait()
+    inner(1).start()
+    border(5).start()
+    wait_load(4)
+    wait_load(5)
     lax.fori_loop(8, 15, sums, 0)
 
-    for d in range(2):
-        lon_static(d).wait_recv()
+    remote(LS, LR, edge_send, edge_recv, sides[0]).wait_recv()
 
     def take(block, carry):
         unpack(0, 9, LR, pl.multiple_of(block * 16, 16), 16)
@@ -327,82 +358,84 @@
 
     lax.fori_loop(0, 16, take, 0)
     for k in range(2):
-        for d in range(2):
-            lon_edge(d, k).wait_recv()
+        wait_columns(248 * k, 8, CHUNKS + k)
         unpack(ST, 3, XR, 248 * k, 8)
     to_rows(2)
-    for c in range(5, BORDERS_AHEAD):
-        inner(c - 3).start()
-        border(c).start()
-    inner(BORDERS_AHEAD - 3).start()
+    for c in range(3):
+        border(2 * c + 6).start()
+        border(2 * c + 7).start()
+        inner(c + 2).start()
+    inner(5).start()
 
     def columns(c):
         row = pl.multiple_of(8 + c * 16, 8)
         border(c).wait_recv()
         totals(range(2), row, 16)
         pack(ST, 3, XS, row, 16)
-        for d in range(2):
-            lon_chunk(d, c).start()
+        start_columns(row, 16, c)
 
     for c in range(COLUMNS_AHEAD):
         columns(c)
 
+    everything = (slice(None), slice(None))
+
     @pl.when(has_down)
     def _():
-        for k in range(3):
-            lat_message(0, k).wait_recv()
-            lat_message(1, k).wait_send()
+        lat_copy(0, *everything).wait_recv()
+        lat_copy(1, *everything).wait_send()
 
     @pl.when(has_up)
     def _():
-        for k in range(3):
-            lat_message(1, k).wait_recv()
-            lat_message(0, k).wait_send()
+        lat_copy(1, *everything).wait_recv()
+        lat_copy(0, *everything).wait_send()
 
     lax.fori_loop(0, 2, step, 0)
+
+    def columns_here(c):
+        row = pl.multiple_of(8 + c * 16, 8)
+        wait_columns(row, 16, c)
+        unpack(ST, 3, XR, row, 16)
 
     def chunk(c, carry):
         @pl.when(c + COLUMNS_AHEAD < CHUNKS)
         def _():
             columns(c + COLUMNS_AHEAD)
 
-        row = pl.multiple_of(8 + c * 16, 8)
-        for d in range(2):
-            lon_chunk(d, c).wait_recv()
-        unpack(ST, 3, XR, row, 16)
+        columns_here(c)
         inner(c).wait_recv()
 
         @pl.when(c + BORDERS_AHEAD < CHUNKS)
         def _():
             border(c + BORDERS_AHEAD).start()
 
-        @pl.when(c + INNERS_AHEAD < CHUNKS)
+        @pl.when(c + INNERS_AHEAD < CHUNKS - 1)
         def _():
             inner(c + INNERS_AHEAD).start()
 
-        totals(range(2, 5), row, 16)
+        @pl.when(c + INNERS_AHEAD == CHUNKS - 1)
+        def _():
+            last_inner(0).start()
+            last_inner(1).start()
+
+        totals(range(2, 5), pl.multiple_of(8 + c * 16, 8), 16)
         lax.fori_loop(2 * c + 2, 2 * c + 4, step, 0)
         return carry
 
-    lax.fori_loop(0, CHUNKS, chunk, 0)
-    lax.fori_loop(32, 34, step, 0)
+    lax.fori_loop(0, CHUNKS - 1, chunk, 0)
+    columns_here(CHUNKS - 1)
+    last_inner(0).wait_recv()
+    totals(range(2, 5), ROWS - 24, 8)
+    lax.fori_loop(30, 31, step, 0)
+    last_inner(1).wait_recv()
+    totals(range(2, 5), ROWS - 16, 8)
+    lax.fori_loop(31, 34, step, 0)
     for t in range(34, 40):
         for lag in range(t - 33, 8):
             half_stage(lag, t + FIRST - lag)
 
-    def finish(c, carry):
-        border(c).wait_send()
-        inner(c).wait_send()
-        for d in range(2):
-            lon_chunk(d, c).wait_send()
-        return carry
-
-    lax.fori_loop(0, CHUNKS, finish, 0)
-    for k in range(2):
-        edge(k).wait_send()
-        lon_static(k).wait_send()
-        for d in range(2):
-            lon_edge(d, k).wait_send()
+    remote(PT, QT, cat_send, cat_recv.at[0], peer).wait_send()
+    remote(XS, XR, lon_send, lon_recv.at[0], sides[0]).wait_send()
+    remote(LS, LR, edge_send, edge_recv, sides[0]).wait_send()
 
 
 def shards(*arrays):
@@ -416,8 +449,7 @@
         scratch_shapes=[
             pltpu.VMEM((12, 6, HEIGHT, 128), f32),
             pltpu.SMEM((NCAT,), f32),
-            pltpu.VMEM((NCAT, ROWS, COLS), jnp.bfloat16),
-            pltpu.VMEM((NCAT, ROWS, COLS), jnp.bfloat16),
+            pltpu.VMEM((2, NCAT, ROWS, COLS), jnp.bfloat16),
             pltpu.VMEM((ROWS, COLS), jnp.int32),
             pltpu.VMEM((ROWS, COLS), jnp.int32),
             pltpu.VMEM((3, TILES, ROWS, 128), f32),
@@ -426,16 +458,18 @@
             pltpu.VMEM((2, ROWS, 128), f32),
             pltpu.VMEM((2, ROWS, 128), f32),
             pltpu.VMEM((2, ROWS, 128), f32),
-            dma((2 * CHUNKS + 2,)),
-            dma((2 * CHUNKS + 2,)),
-            dma((CHUNKS + 2, 2)),
-            dma((CHUNKS + 2, 2)),
+            dma,
+            dma((2 * CHUNKS + 3,)),
+            dma,
+            dma((CHUNKS + 2,)),
+            dma,
+            dma,
             dma((2,)),
             dma((2,)),
-            dma((3, 2)),
-            dma((3, 2)),
-            dma((len(LOADS), 3)),
-            dma((9, TILES)),
+            dma((len(LOADS),)),
+            dma((len(TOPS),)),
+            dma((3,)),
+            pltpu.SemaphoreType.REGULAR,
         ],
         compiler_params=pltpu.CompilerParams(
             collective_id=0, has_side_effects=True, vmem_limit_bytes=44 * 2**20

time: 63.7 us -> 59.4 us (0.932)
  the two profiles are of different devices: /device:TPU:2 before, /device:TPU:1 now
where the time goes in v3:
time: 59.4 us; the launch traced here: 59 us
  Pallas kernels  56.6 us (95%)
  local copies, waits for them, and re-layouts  1.74 us (3%)
  between operations  0.64 us (1%)
    pallas_call x1, Pallas kernels, shards(): pl.pallas_call(kernel, out_shape=jax.ShapeDtypeStruct((5, ROWS, COLS), f3...  56.6 us
    squeeze x1, local copies, waits for them, and re-layouts, shards(): return tuple((result[i] for i in range(5)))  1.74 us

profile of v3, /device:TPU:1, one launch (start us, length us, event | category | flops | bytes accessed | tf_op | source)
XLA Modules:
  0.0 59.0 jit_solution(6375659839698896877)
XLA Ops:
  0.6 56.6 %ice.1 = f32[5,256,640]{2,1,0:T(8,128)S(1)} custom-call(bf16[20,256,640]{2,1,0:T(8,128)(2,1)} %th.1, bf16[20,256,640]{2,1,0:T(8,128)(2,1)} %ar.1, f32[20]{0:T(128)} %weight.1, s32[256,640]{1,0:T(8,128)} %top.1, s32[256,640]{1,0:T(8,128)} %land.1, f32[256,640]{1,0:T(8,128)} %u0.1, f32[256,640]{1,0:T(8,128)} %v0.1, f32[256,640]{1,0:T(8,128)} %d0.1, ...), custom_call_target="tpu_custom_call" | custom-call | tf_op jit(solution)/shard_map/ice/pallas_call | solution.py:444
  57.3 1.7 %slice_bitcast_fusion = (f32[256,640]{1,0:T(8,128)}, f32[256,640]{1,0:T(8,128)}, f32[256,640]{1,0:T(8,128)}, f32[256,640]{1,0:T(8,128)}, f32[256,640]{1,0:T(8,128)}) fusion(f32[5,256,640]{2,1,0:T(8,128)S(1)} %ice.1), kind=kLoop, calls=%fused_computation | loop fusion | bytes 6553600 | tf_op jit(solution)/shard_map/squeeze | solution.py:479

commit v4 on v3

--- a/solution.py
+++ b/solution.py
@@ -32,6 +32,8 @@
     sides = ((cat, lat, lax.rem(lon + 15, 16)), (cat, lat, lax.rem(lon + 1, 16)))
     up = (cat, lax.rem(lat + 3, 4), lon)
     down = (cat, lax.rem(lat + 1, 4), lon)
+    cross_up = (1 - cat, lax.rem(lat + 3, 4), lon)
+    cross_down = (1 - cat, lax.rem(lat + 1, 4), lon)
     has_up, has_down = lat > 0, lat < 3
 
     even = lax.rem(lon, 2) == 0
@@ -74,7 +76,7 @@
     weights.start()
     start_load(1)
     barrier = pltpu.get_barrier_semaphore()
-    for device in (peer, up, down):
+    for device in (peer, up, down, cross_up, cross_down):
         pl.semaphore_signal(barrier, inc=1, device_id=device, device_id_type=MESH)
 
     @pl.when(even)
@@ -85,11 +87,11 @@
     def enter():
         @pl.when(even)
         def _():
-            pl.semaphore_wait(barrier, 3)
+            pl.semaphore_wait(barrier, 5)
 
         @pl.when(jnp.logical_not(even))
         def _():
-            pl.semaphore_wait(barrier, 5)
+            pl.semaphore_wait(barrier, 7)
             for device in sides:
                 pl.semaphore_signal(near, inc=1, device_id=device, device_id_type=MESH)
 
@@ -159,18 +161,33 @@
         rows = pl.ds(start, size)
         remote(XS.at[:, rows, :], XR.at[:, rows, :], lon_send, lon_recv.at[k], sides[0]).wait_recv()
 
-    def lat_message(d, k):
-        fields, tiles = (
-            (pl.ds(0, 9), pl.ds(0, TILES)), (pl.ds(9, 3), pl.ds(0, TILES)), (pl.ds(0, 12), pl.ds(TILES, 1))
-        )[k]
-        return lat_copy(d, fields, tiles)
-
-    def lat_copy(d, fields, tiles):
-        here, there, device = ((FIRST + 1, LAST, up), (LAST - 1, FIRST, down))[d]
+    def lat_copy(d, fields, tiles, over=False):
+        here, there, device = ((FIRST + 1, LAST, (up, cross_up)[over]), (LAST - 1, FIRST, (down, cross_down)[over]))[d]
         return remote(
             F.at[fields, tiles, pl.ds(8 * here, 8), :], F.at[fields, tiles, pl.ds(8 * there, 8), :],
             lat_send.at[d], lat_recv.at[d], device,
         )
+
+    def to_rows(k):
+        fields = (pl.ds(0, 9), pl.ds(9, 3), pl.ds(0, 12))[k]
+        corner = pl.ds(TILES, 1)
+        for d in range(2):
+            crosses = lat == (2, 1)[d]
+
+            @pl.when((has_up, has_down)[d] & jnp.logical_not(crosses))
+            def _():
+                lat_copy(d, fields, corner if k == 2 else pl.ds(0, TILES)).start()
+
+            if k < 2:
+                @pl.when(crosses & (cat == 0))
+                def _():
+                    for over in range(2):
+                        lat_copy(d, fields, pl.ds(0, 3), over).start()
+
+            @pl.when(crosses & (cat == 1))
+            def _():
+                for over in range(2):
+                    lat_copy(d, fields, corner if k == 2 else pl.ds(3, 2), over).start()
 
     def pack(first, count, send, row, size):
         iota = lane if size == 8 else lane16
@@ -224,6 +241,7 @@
             F[WY, j, rows, :] = push * F[WY, j, rows, :]
             F[DR, j, rows, :] = 0.25 * g
             F[WT, j, rows, :] = wet * (1.0 / 3.0)
+            F[ST, j, rows, :] = (wet * (2.0 / 3.0)) * F[ST, j, rows, :]
 
     def stress(band, last=None):
         row = pl.multiple_of(8 * band, 8)
@@ -235,14 +253,14 @@
             uy = F[U, j, below, :] - F[U, j, above, :]
             vy = F[V, j, below, :] - F[V, j, above, :]
             div, ten, shr = ux + vy, ux - vy, uy + vx
-            square = 0.25 * (div * div + 0.25 * (ten * ten + shr * shr)) + 0.0025
+            square = div * div + 0.25 * (ten * ten + shr * shr) + 0.01
             strength = F[ST, j, rows, :]
             half = strength * lax.rsqrt(square)
             eighth = 0.25 * half
             third = F[WT, j, rows, :]
-            s1 = third * (F[S1, j, rows, :] + half * div - 2.0 * strength)
-            s2 = third * (F[S2, j, rows, :] + eighth * ten)
-            s12 = third * (F[S12, j, rows, :] + eighth * shr)
+            s1 = third * F[S1, j, rows, :] + (half * div - strength)
+            s2 = third * F[S2, j, rows, :] + eighth * ten
+            s12 = third * F[S12, j, rows, :] + eighth * shr
             F[S1, j, rows, :] = s1
             F[S2, j, rows, :] = s2
             F[S12, j, rows, :] = s12
@@ -327,15 +345,6 @@
     for d in range(2):
         remote(LS.at[d], LR.at[d], edge_send, edge_recv, sides[d]).start()
 
-    def to_rows(k):
-        @pl.when(has_up)
-        def _():
-            lat_message(0, k).start()
-
-        @pl.when(has_down)
-        def _():
-            lat_message(1, k).start()
-
     to_rows(0)
 
     for k in range(2):
@@ -350,6 +359,9 @@
     wait_load(5)
     lax.fori_loop(8, 15, sums, 0)
 
+    border(6).start()
+    border(7).start()
+    inner(2).start()
     remote(LS, LR, edge_send, edge_recv, sides[0]).wait_recv()
 
     def take(block, carry):
@@ -361,10 +373,10 @@
         wait_columns(248 * k, 8, CHUNKS + k)
         unpack(ST, 3, XR, 248 * k, 8)
     to_rows(2)
-    for c in range(3):
-        border(2 * c + 6).start()
-        border(2 * c + 7).start()
-        inner(c + 2).start()
+    for c in range(2):
+        border(2 * c + 8).start()
+        border(2 * c + 9).start()
+        inner(c + 3).start()
     inner(5).start()
 
     def columns(c):

time: 59.4 us -> 66.3 us (1.12)
  Pallas kernels: 56.6 us -> 63.8 us
    pallas_call x1, Pallas kernels: 56.6 us -> 63.8 us  [shards(): pl.pallas_call(kernel, out_shape=jax.ShapeDtypeStruct((5, ROWS, COLS), f3...]
where the time goes in v4:
time: 66.3 us; the launch traced here: 66.2 us
  Pallas kernels  63.8 us (96%)
  local copies, waits for them, and re-layouts  1.74 us (3%)
    pallas_call x1, Pallas kernels, shards(): pl.pallas_call(kernel, out_shape=jax.ShapeDtypeStruct((5, ROWS, COLS), f3...  63.8 us
    squeeze x1, local copies, waits for them, and re-layouts, shards(): return tuple((result[i] for i in range(5)))  1.74 us

profile of v4, /device:TPU:1, one launch (start us, length us, event | category | flops | bytes accessed | tf_op | source)
XLA Modules:
  0.0 66.2 jit_solution(16728940501319724687)
XLA Ops:
  0.6 63.8 %ice.1 = f32[5,256,640]{2,1,0:T(8,128)S(1)} custom-call(bf16[20,256,640]{2,1,0:T(8,128)(2,1)} %th.1, bf16[20,256,640]{2,1,0:T(8,128)(2,1)} %ar.1, f32[20]{0:T(128)} %weight.1, s32[256,640]{1,0:T(8,128)} %top.1, s32[256,640]{1,0:T(8,128)} %land.1, f32[256,640]{1,0:T(8,128)} %u0.1, f32[256,640]{1,0:T(8,128)} %v0.1, f32[256,640]{1,0:T(8,128)} %d0.1, ...), custom_call_target="tpu_custom_call" | custom-call | tf_op jit(solution)/shard_map/ice/pallas_call | solution.py:456
  64.4 1.7 %slice_bitcast_fusion = (f32[256,640]{1,0:T(8,128)}, f32[256,640]{1,0:T(8,128)}, f32[256,640]{1,0:T(8,128)}, f32[256,640]{1,0:T(8,128)}, f32[256,640]{1,0:T(8,128)}) fusion(f32[5,256,640]{2,1,0:T(8,128)S(1)} %ice.1), kind=kLoop, calls=%fused_computation | loop fusion | bytes 6553600 | tf_op jit(solution)/shard_map/squeeze | solution.py:491

commit v5 on v4

--- a/solution.py
+++ b/solution.py
@@ -24,8 +24,8 @@
 
 
 def kernel(th, ar, weight, top, land, u0, v0, d0, t0, h0, wx0, wy0, dr0, out,
-           F, W, TA, TOP, LAND, PT, QT, LS, LR, XS, XR,
-           cat_send, cat_recv, lon_send, lon_recv, edge_send, edge_recv, lat_send, lat_recv,
+           F, W, TA, TOP, LAND, PT, QT, LS, LR, XS, XR, HS, HR,
+           cat_send, cat_recv, lon_send, lon_recv, edge_send, edge_recv, lat_send, lat_recv, halo_send, halo_recv,
            load_sem, top_sem, field_sem, near):
     cat, lat, lon = lax.axis_index("cat"), lax.axis_index("lat"), lax.axis_index("lon")
     peer = (1 - cat, lat, lon)
@@ -169,29 +169,28 @@
         )
 
     def to_rows(k):
-        fields = (pl.ds(0, 9), pl.ds(9, 3), pl.ds(0, 12))[k]
-        corner = pl.ds(TILES, 1)
+        fields = (pl.ds(0, 9), pl.ds(9, 3))[k]
+        halves = (
+            (((pl.ds(0, 9), pl.ds(0, 2)), (pl.ds(0, 6), pl.ds(2, 1))), ((pl.ds(0, 9), pl.ds(3, 2)), (pl.ds(6, 3), pl.ds(2, 1)))),
+            (((pl.ds(9, 3), pl.ds(0, 2)),), ((pl.ds(9, 3), pl.ds(2, 3)),)),
+        )[k]
         for d in range(2):
             crosses = lat == (2, 1)[d]
 
             @pl.when((has_up, has_down)[d] & jnp.logical_not(crosses))
             def _():
-                lat_copy(d, fields, corner if k == 2 else pl.ds(0, TILES)).start()
-
-            if k < 2:
-                @pl.when(crosses & (cat == 0))
+                lat_copy(d, fields, pl.ds(0, TILES)).start()
+
+            for holder in range(2):
+                @pl.when(crosses & (cat == holder))
                 def _():
-                    for over in range(2):
-                        lat_copy(d, fields, pl.ds(0, 3), over).start()
-
-            @pl.when(crosses & (cat == 1))
-            def _():
-                for over in range(2):
-                    lat_copy(d, fields, corner if k == 2 else pl.ds(3, 2), over).start()
-
-    def pack(first, count, send, row, size):
+                    for some, tiles in halves[holder]:
+                        for over in range(2):
+                            lat_copy(d, some, tiles, over).start()
+
+    def pack(first, count, send, row, size, place=None):
         iota = lane if size == 8 else lane16
-        rows = pl.ds(row, size)
+        rows = pl.ds(row if place is None else place, size)
         from_rows = pl.ds(row + TOP_ROW, size)
         left = jnp.zeros((size, 128), jnp.float32)
         right = jnp.zeros((size, 128), jnp.float32)
@@ -204,9 +203,9 @@
         send[0, rows, :] = left
         send[1, rows, :] = right
 
-    def unpack(first, count, recv, row, size):
+    def unpack(first, count, recv, row, size, place=None):
         iota = lane if size == 8 else lane16
-        rows = pl.ds(row, size)
+        rows = pl.ds(row if place is None else place, size)
         a = recv[0, rows, :]
         b = recv[1, rows, :]
         for i in range(count):
@@ -359,9 +358,11 @@
     wait_load(5)
     lax.fori_loop(8, 15, sums, 0)
 
-    border(6).start()
-    border(7).start()
-    inner(2).start()
+    for c in range(3):
+        border(2 * c + 6).start()
+        border(2 * c + 7).start()
+        inner(c + 2).start()
+    inner(5).start()
     remote(LS, LR, edge_send, edge_recv, sides[0]).wait_recv()
 
     def take(block, carry):
@@ -372,12 +373,6 @@
     for k in range(2):
         wait_columns(248 * k, 8, CHUNKS + k)
         unpack(ST, 3, XR, 248 * k, 8)
-    to_rows(2)
-    for c in range(2):
-        border(2 * c + 8).start()
-        border(2 * c + 9).start()
-        inner(c + 3).start()
-    inner(5).start()
 
     def columns(c):
         row = pl.multiple_of(8 + c * 16, 8)
@@ -386,21 +381,29 @@
         pack(ST, 3, XS, row, 16)
         start_columns(row, 16, c)
 
-    for c in range(COLUMNS_AHEAD):
+    for c in range(3):
         columns(c)
-
-    everything = (slice(None), slice(None))
+    halo = (slice(None), pl.ds(0, TILES))
 
     @pl.when(has_down)
     def _():
-        lat_copy(0, *everything).wait_recv()
-        lat_copy(1, *everything).wait_send()
+        lat_copy(0, *halo).wait_recv()
+        lat_copy(1, *halo).wait_send()
 
     @pl.when(has_up)
     def _():
-        lat_copy(1, *everything).wait_recv()
-        lat_copy(0, *everything).wait_send()
-
+        lat_copy(1, *halo).wait_recv()
+        lat_copy(0, *halo).wait_send()
+
+    for k in range(2):
+        pack(0, 12, HS, (-8, ROWS)[k], 8, 8 * k)
+    for d in range(2):
+        remote(HS.at[d], HR.at[d], halo_send, halo_recv, sides[d]).start()
+    for c in range(3, COLUMNS_AHEAD):
+        columns(c)
+    remote(HS, HR, halo_send, halo_recv, sides[0]).wait_recv()
+    for k in range(2):
+        unpack(0, 12, HR, (-8, ROWS)[k], 8, 8 * k)
     lax.fori_loop(0, 2, step, 0)
 
     def columns_here(c):
@@ -448,6 +451,7 @@
     remote(PT, QT, cat_send, cat_recv.at[0], peer).wait_send()
     remote(XS, XR, lon_send, lon_recv.at[0], sides[0]).wait_send()
     remote(LS, LR, edge_send, edge_recv, sides[0]).wait_send()
+    remote(HS, HR, halo_send, halo_recv, sides[0]).wait_send()
 
 
 def shards(*arrays):
@@ -470,6 +474,8 @@
             pltpu.VMEM((2, ROWS, 128), f32),
             pltpu.VMEM((2, ROWS, 128), f32),
             pltpu.VMEM((2, ROWS, 128), f32),
+            pltpu.VMEM((2, 16, 128), f32),
+            pltpu.VMEM((2, 16, 128), f32),
             dma,
             dma((2 * CHUNKS + 3,)),
             dma,
@@ -478,6 +484,8 @@
             dma,
             dma((2,)),
             dma((2,)),
+            dma,
+            dma,
             dma((len(LOADS),)),
             dma((len(TOPS),)),
             dma((3,)),

time: 66.3 us -> 55 us (0.83)
  Pallas kernels: 63.8 us -> 52.5 us
    pallas_call x1, Pallas kernels: 63.8 us -> 52.5 us  [shards(): pl.pallas_call(kernel, out_shape=jax.ShapeDtypeStruct((5, ROWS, COLS), f3...]
where the time goes in v5:
time: 55 us; the launch traced here: 54.9 us
  Pallas kernels  52.5 us (95%)
  local copies, waits for them, and re-layouts  1.74 us (3%)
  between operations  0.64 us (1%)
    pallas_call x1, Pallas kernels, shards(): pl.pallas_call(kernel, out_shape=jax.ShapeDtypeStruct((5, ROWS, COLS), f3...  52.5 us
    squeeze x1, local copies, waits for them, and re-layouts, shards(): return tuple((result[i] for i in range(5)))  1.74 us

profile of v5, /device:TPU:1, one launch (start us, length us, event | category | flops | bytes accessed | tf_op | source)
XLA Modules:
  0.0 54.9 jit_solution(1294334463697040056)
XLA Ops:
  0.6 52.5 %ice.1 = f32[5,256,640]{2,1,0:T(8,128)S(1)} custom-call(bf16[20,256,640]{2,1,0:T(8,128)(2,1)} %th.1, bf16[20,256,640]{2,1,0:T(8,128)(2,1)} %ar.1, f32[20]{0:T(128)} %weight.1, s32[256,640]{1,0:T(8,128)} %top.1, s32[256,640]{1,0:T(8,128)} %land.1, f32[256,640]{1,0:T(8,128)} %u0.1, f32[256,640]{1,0:T(8,128)} %v0.1, f32[256,640]{1,0:T(8,128)} %d0.1, ...), custom_call_target="tpu_custom_call" | custom-call | tf_op jit(solution)/shard_map/ice/pallas_call | solution.py:460
  53.1 1.7 %slice_bitcast_fusion = (f32[256,640]{1,0:T(8,128)}, f32[256,640]{1,0:T(8,128)}, f32[256,640]{1,0:T(8,128)}, f32[256,640]{1,0:T(8,128)}, f32[256,640]{1,0:T(8,128)}) fusion(f32[5,256,640]{2,1,0:T(8,128)S(1)} %ice.1), kind=kLoop, calls=%fused_computation | loop fusion | bytes 6553600 | tf_op jit(solution)/shard_map/squeeze | solution.py:499

commit v6 on v5

--- a/solution.py
+++ b/solution.py
@@ -76,8 +76,12 @@
     weights.start()
     start_load(1)
     barrier = pltpu.get_barrier_semaphore()
-    for device in (peer, up, down, cross_up, cross_down):
-        pl.semaphore_signal(barrier, inc=1, device_id=device, device_id_type=MESH)
+    pl.semaphore_signal(barrier, inc=1, device_id=peer, device_id_type=MESH)
+    inside = (lat == 1) | (lat == 2)
+    for there, device in ((has_up, up), (has_down, down), (lat == 2, cross_up), (lat == 1, cross_down)):
+        @pl.when(there)
+        def _():
+            pl.semaphore_signal(barrier, inc=1, device_id=device, device_id_type=MESH)
 
     @pl.when(even)
     def _():
@@ -85,13 +89,21 @@
             pl.semaphore_signal(barrier, inc=1, device_id=device, device_id_type=MESH)
 
     def enter():
-        @pl.when(even)
-        def _():
-            pl.semaphore_wait(barrier, 5)
+        for middle in range(2):
+            @pl.when(inside == bool(middle))
+            def _():
+                partners = 4 if middle else 2
+
+                @pl.when(even)
+                def _():
+                    pl.semaphore_wait(barrier, partners)
+
+                @pl.when(jnp.logical_not(even))
+                def _():
+                    pl.semaphore_wait(barrier, partners + 2)
 
         @pl.when(jnp.logical_not(even))
         def _():
-            pl.semaphore_wait(barrier, 7)
             for device in sides:
                 pl.semaphore_signal(near, inc=1, device_id=device, device_id_type=MESH)
 
@@ -140,17 +152,30 @@
         where = (slice(None), tiles, rows, slice(None))
         return remote(PT.at[where], QT.at[where], cat_send, cat_recv.at[k], peer)
 
+    def sixteen(c):
+        return pl.ds(pl.multiple_of(8 + c * 16, 8), 16)
+
     def border(c):
-        return cat_message(pl.ds(0, 2), pl.ds(pl.multiple_of(8 + c * 16, 8), 16), c)
+        first = isinstance(c, int) and c < COLUMNS_AHEAD
+        return cat_message(pl.ds(0, 2), sixteen(c), CHUNKS + 1 + c // 3 if first else c - COLUMNS_AHEAD)
 
     def inner(c):
-        return cat_message(pl.ds(2, 3), pl.ds(pl.multiple_of(8 + c * 16, 8), 16), CHUNKS + c)
+        return cat_message(pl.ds(2, 3), sixteen(c), c)
 
     def last_inner(k):
-        return cat_message(pl.ds(2, 3), pl.ds(ROWS - 24 + 8 * k, 8), 2 * CHUNKS - 1 + k)
+        return cat_message(pl.ds(2, 3), pl.ds(ROWS - 24 + 8 * k, 8), CHUNKS - 1 + k)
 
     def edge(k):
-        return cat_message(pl.ds(0, 5), pl.ds(248 * k, 8), 2 * CHUNKS + 1 + k)
+        return cat_message(pl.ds(0, 5), pl.ds(248 * k, 8), CHUNKS + 3)
+
+    def wait_first_borders(group):
+        cat_message(pl.ds(0, 2), pl.ds(8, 48), CHUNKS + 1 + group).wait_recv()
+
+    def wait_edges():
+        cat_message(pl.ds(0, 5), pl.ds(0, 16), CHUNKS + 3).wait_recv()
+
+    def wait_both(c):
+        cat_message(pl.ds(0, 5), sixteen(c), c).wait_recv()
 
     def start_columns(start, size, k):
         rows = pl.ds(start, size)
@@ -346,11 +371,11 @@
 
     to_rows(0)
 
+    wait_edges()
     for k in range(2):
-        edge(k).wait_recv()
         totals(range(5), 248 * k, 8)
         pack(ST, 3, XS, 248 * k, 8)
-        start_columns(248 * k, 8, CHUNKS + k)
+        start_columns(248 * k, 8, CHUNKS)
     to_rows(1)
     inner(1).start()
     border(5).start()
@@ -370,17 +395,17 @@
         return carry
 
     lax.fori_loop(0, 16, take, 0)
+    wait_columns(0, 16, CHUNKS)
     for k in range(2):
-        wait_columns(248 * k, 8, CHUNKS + k)
         unpack(ST, 3, XR, 248 * k, 8)
 
     def columns(c):
         row = pl.multiple_of(8 + c * 16, 8)
-        border(c).wait_recv()
         totals(range(2), row, 16)
         pack(ST, 3, XS, row, 16)
         start_columns(row, 16, c)
 
+    wait_first_borders(0)
     for c in range(3):
         columns(c)
     halo = (slice(None), pl.ds(0, TILES))
@@ -399,6 +424,7 @@
         pack(0, 12, HS, (-8, ROWS)[k], 8, 8 * k)
     for d in range(2):
         remote(HS.at[d], HR.at[d], halo_send, halo_recv, sides[d]).start()
+    wait_first_borders(1)
     for c in range(3, COLUMNS_AHEAD):
         columns(c)
     remote(HS, HR, halo_send, halo_recv, sides[0]).wait_recv()
@@ -414,10 +440,14 @@
     def chunk(c, carry):
         @pl.when(c + COLUMNS_AHEAD < CHUNKS)
         def _():
+            wait_both(c)
             columns(c + COLUMNS_AHEAD)
 
+        @pl.when(c + COLUMNS_AHEAD >= CHUNKS)
+        def _():
+            inner(c).wait_recv()
+
         columns_here(c)
-        inner(c).wait_recv()
 
         @pl.when(c + BORDERS_AHEAD < CHUNKS)
         def _():
@@ -441,12 +471,17 @@
     last_inner(0).wait_recv()
     totals(range(2, 5), ROWS - 24, 8)
     lax.fori_loop(30, 31, step, 0)
+    for band in (LAST - 1, LAST):
+        coefficients(band)
+        half_stage(0, band)
+    half_stage(1, LAST)
     last_inner(1).wait_recv()
     totals(range(2, 5), ROWS - 16, 8)
-    lax.fori_loop(31, 34, step, 0)
-    for t in range(34, 40):
-        for lag in range(t - 33, 8):
-            half_stage(lag, t + FIRST - lag)
+    lax.fori_loop(31, 32, step, 0)
+    for t in range(32, 40):
+        for lag in range(max(1, t - 33), 8):
+            if (t, lag) != (34, 1):
+                half_stage(lag, t + FIRST - lag)
 
     remote(PT, QT, cat_send, cat_recv.at[0], peer).wait_send()
     remote(XS, XR, lon_send, lon_recv.at[0], sides[0]).wait_send()
@@ -477,9 +512,9 @@
             pltpu.VMEM((2, 16, 128), f32),
             pltpu.VMEM((2, 16, 128), f32),
             dma,
-            dma((2 * CHUNKS + 3,)),
+            dma((CHUNKS + 4,)),
             dma,
-            dma((CHUNKS + 2,)),
+            dma((CHUNKS + 1,)),
             dma,
             dma,
             dma((2,)),

time: 55 us -> 54.7 us (level)
  no operation moved by 1% of the time
where the time goes in v6:
time: 54.7 us; the launch traced here: 54.6 us
  Pallas kernels  52.2 us (95%)
  local copies, waits for them, and re-layouts  1.74 us (3%)
  between operations  0.64 us (1%)
    pallas_call x1, Pallas kernels, shards(): pl.pallas_call(kernel, out_shape=jax.ShapeDtypeStruct((5, ROWS, COLS), f3...  52.2 us
    squeeze x1, local copies, waits for them, and re-layouts, shards(): return tuple((result[i] for i in range(5)))  1.74 us

profile of v6, /device:TPU:1, one launch (start us, length us, event | category | flops | bytes accessed | tf_op | source)
XLA Modules:
  0.0 54.6 jit_solution(9502185908125361831)
XLA Ops:
  0.6 52.2 %ice.1 = f32[5,256,640]{2,1,0:T(8,128)S(1)} custom-call(bf16[20,256,640]{2,1,0:T(8,128)(2,1)} %th.1, bf16[20,256,640]{2,1,0:T(8,128)(2,1)} %ar.1, f32[20]{0:T(128)} %weight.1, s32[256,640]{1,0:T(8,128)} %top.1, s32[256,640]{1,0:T(8,128)} %land.1, f32[256,640]{1,0:T(8,128)} %u0.1, f32[256,640]{1,0:T(8,128)} %v0.1, f32[256,640]{1,0:T(8,128)} %d0.1, ...), custom_call_target="tpu_custom_call" | custom-call | tf_op jit(solution)/shard_map/ice/pallas_call | solution.py:495
  52.9 1.7 %slice_bitcast_fusion = (f32[256,640]{1,0:T(8,128)}, f32[256,640]{1,0:T(8,128)}, f32[256,640]{1,0:T(8,128)}, f32[256,640]{1,0:T(8,128)}, f32[256,640]{1,0:T(8,128)}) fusion(f32[5,256,640]{2,1,0:T(8,128)S(1)} %ice.1), kind=kLoop, calls=%fused_computation | loop fusion | bytes 6553600 | tf_op jit(solution)/shard_map/squeeze | solution.py:534

commit v7 on v6

--- a/solution.py
+++ b/solution.py
@@ -377,11 +377,22 @@
         pack(ST, 3, XS, 248 * k, 8)
         start_columns(248 * k, 8, CHUNKS)
     to_rows(1)
-    inner(1).start()
-    border(5).start()
+
+    @pl.when(inside)
+    def _():
+        inner(1).start()
+        border(5).start()
+
     wait_load(4)
     wait_load(5)
     lax.fori_loop(8, 15, sums, 0)
+
+
+    @pl.when(jnp.logical_not(inside))
+    def _():
+        pl.delay(1700)
+        inner(1).start()
+        border(5).start()
 
     for c in range(3):
         border(2 * c + 6).start()

time: 54.7 us -> 53.8 us (0.984); the launches traced: 54.6 us -> 53.1 us
  Pallas kernels: 52.2 us -> 50.7 us
    pallas_call x1, Pallas kernels: 52.2 us -> 50.7 us  [shards(): pl.pallas_call(kernel, out_shape=jax.ShapeDtypeStruct((5, ROWS, COLS), f3...]
where the time goes in v7:
time: 53.8 us; the launch traced here: 53.1 us
  Pallas kernels  50.7 us (94%)
  local copies, waits for them, and re-layouts  1.74 us (3%)
  between operations  0.64 us (1%)
    pallas_call x1, Pallas kernels, shards(): pl.pallas_call(kernel, out_shape=jax.ShapeDtypeStruct((5, ROWS, COLS), f3...  50.7 us
    squeeze x1, local copies, waits for them, and re-layouts, shards(): return tuple((result[i] for i in range(5)))  1.74 us

profile of v7, /device:TPU:1, one launch (start us, length us, event | category | flops | bytes accessed | tf_op | source)
XLA Modules:
  0.0 53.1 jit_solution(13877765371093304170)
XLA Ops:
  0.6 50.7 %ice.1 = f32[5,256,640]{2,1,0:T(8,128)S(1)} custom-call(bf16[20,256,640]{2,1,0:T(8,128)(2,1)} %th.1, bf16[20,256,640]{2,1,0:T(8,128)(2,1)} %ar.1, f32[20]{0:T(128)} %weight.1, s32[256,640]{1,0:T(8,128)} %top.1, s32[256,640]{1,0:T(8,128)} %land.1, f32[256,640]{1,0:T(8,128)} %u0.1, f32[256,640]{1,0:T(8,128)} %v0.1, f32[256,640]{1,0:T(8,128)} %d0.1, ...), custom_call_target="tpu_custom_call" | custom-call | tf_op jit(solution)/shard_map/ice/pallas_call | solution.py:506
  51.3 1.7 %slice_bitcast_fusion = (f32[256,640]{1,0:T(8,128)}, f32[256,640]{1,0:T(8,128)}, f32[256,640]{1,0:T(8,128)}, f32[256,640]{1,0:T(8,128)}, f32[256,640]{1,0:T(8,128)}) fusion(f32[5,256,640]{2,1,0:T(8,128)S(1)} %ice.1), kind=kLoop, calls=%fused_computation | loop fusion | bytes 6553600 | tf_op jit(solution)/shard_map/squeeze | solution.py:545
